TPU v7x, 16 devices: a whole 2x2x2 slice. The times are simulated.
16 devices in a mesh: rep: 4 (over z, y), ep: 4 (over x, core).
Axes of the slice: x: 2, y: 2, z: 2, core: 2. Of those that a mesh axis runs over, the one named last changes fastest.
Arguments:
- x: bfloat16 [1024, 2048], P(('rep', 'ep')), parts along dimension 0
- cache: bfloat16 [1024, 256, 576], P(('rep', 'ep')), parts along dimension 0
- lens: int32 [1024], P(('rep', 'ep')), parts along dimension 0
- ids: int32 [1024, 6], P(('rep', 'ep')), parts along dimension 0
- rw: float32 [1024, 6], P(('rep', 'ep')), parts along dimension 0
- w_q: bfloat16 [2048, 3072], replicated
- w_dkv: bfloat16 [2048, 576], replicated
- w_uk: bfloat16 [16, 128, 512], replicated
- w_uv: bfloat16 [16, 512, 128], replicated
- w_o: bfloat16 [2048, 2048], replicated
- s_gate: bfloat16 [2048, 2816], replicated
- s_up: bfloat16 [2048, 2816], replicated
- s_down: bfloat16 [2816, 2048], replicated
- e_gate: bfloat16 [64, 2048, 1408], P('ep')
- e_up: bfloat16 [64, 2048, 1408], P('ep')
- e_down: bfloat16 [64, 1408, 2048], P('ep')
Outputs:
- output 1: bfloat16 [1024, 2048], P(('rep', 'ep')), parts along dimension 0
- output 2: bfloat16 [1024, 576], P(('rep', 'ep')), parts along dimension 0
There are 4 independent parts. A program takes and returns all parts, laid end to end along the dimension named above; an argument that names none is the same for every part.
All inputs are finite; a program needn't handle non-finite values.
Results may differ from a plain program's by a relative error of at most 0.0119234.
Values are sent between devices in bfloat16 or wider.
A program may use at most 1.5 GiB of HBM per device.

v0:
```python
import jax
import jax.numpy as jnp
from jax import lax
from jax.sharding import PartitionSpec as P, NamedSharding

EPS = 1e-6
ROPE_BASE = 1.0e4
CAP_FACTOR = 2


def rms(v):
    v = v.astype(jnp.float32)
    return v * lax.rsqrt(jnp.mean(v * v, axis=-1, keepdims=True) + EPS)


def rope(v, pos):
    half = v.shape[-1] // 2
    inv = ROPE_BASE ** (-2.0 * jnp.arange(half, dtype=jnp.float32) / v.shape[-1])
    ang = pos.astype(jnp.float32)[..., None] * inv
    cs = jnp.cos(ang)
    sn = jnp.sin(ang)
    v1 = v[..., :half]
    v2 = v[..., half:]
    return jnp.concatenate([v1 * cs - v2 * sn, v2 * cs + v1 * sn], axis=-1)


def swiglu(u, wg, wu, wd):
    g = jnp.dot(u, wg, preferred_element_type=jnp.float32)
    v = jnp.dot(u, wu, preferred_element_type=jnp.float32)
    return jnp.dot((jax.nn.silu(g) * v).astype(jnp.bfloat16), wd, preferred_element_type=jnp.float32)


def route(col, w, n_col, cap):
    bsz, top = col.shape
    hit = (col[:, :, None] == jnp.arange(n_col)[None, None, :]).astype(jnp.bfloat16)
    flat = hit.reshape(bsz * top, n_col)
    idx = jnp.arange(bsz * top)
    low = (idx[:, None] > idx[None, :]).astype(jnp.bfloat16)
    before = jnp.dot(low, flat, preferred_element_type=jnp.float32)
    rank = jnp.sum(before * flat.astype(jnp.float32), axis=1).astype(jnp.int32).reshape(bsz, top)
    at = (rank[:, :, None] == jnp.arange(cap)[None, None, :]).astype(jnp.bfloat16)
    disp = jnp.einsum('bke,bkr->ber', hit, at, preferred_element_type=jnp.float32).astype(jnp.bfloat16).reshape(bsz, n_col * cap)
    w = w.astype(jnp.float32)
    w1 = w.astype(jnp.bfloat16)
    r1 = w - w1.astype(jnp.float32)
    w2 = r1.astype(jnp.bfloat16)
    w3 = (r1 - w2.astype(jnp.float32)).astype(jnp.bfloat16)
    hw = jnp.stack([w1, w2, w3])[:, :, :, None] * hit[None]
    comb = jnp.einsum('jbke,bkr->jber', hw, at, preferred_element_type=jnp.float32).astype(jnp.bfloat16).reshape(-1, n_col * cap)
    return disp, comb


def attention(x, cache, lens, w_q, w_dkv, w_uk, w_uv, w_o):
    bsz = x.shape[0]
    heads, nope, kvl = w_uk.shape
    kvd = cache.shape[2]
    vh = w_uv.shape[2]
    qkd = nope + kvd - kvl
    xn = rms(x).astype(jnp.bfloat16)
    q = jnp.dot(xn, w_q, preferred_element_type=jnp.float32).astype(jnp.bfloat16).reshape(bsz, heads, qkd)
    kv = jnp.dot(xn, w_dkv, preferred_element_type=jnp.float32)
    kv_new = jnp.concatenate([rms(kv[:, :kvl]), rope(kv[:, kvl:], lens)], axis=-1).astype(jnp.bfloat16)
    q_lat = jnp.einsum('bhd,hdc->bhc', q[:, :, :nope], w_uk, preferred_element_type=jnp.float32).astype(jnp.bfloat16)
    q_rot = rope(q[:, :, nope:].astype(jnp.float32), lens[:, None]).astype(jnp.bfloat16)
    qf = jnp.concatenate([q_lat, q_rot], axis=-1)
    scale = qkd ** -0.5
    s = jnp.einsum('bhc,blc->bhl', qf, cache, preferred_element_type=jnp.float32) * scale
    live = jnp.arange(cache.shape[1])[None, None, :] < lens[:, None, None]
    s = jnp.where(live, s, -jnp.inf)
    s_new = jnp.einsum('bhc,bc->bh', qf, kv_new, preferred_element_type=jnp.float32) * scale
    mx = jnp.maximum(jnp.max(s, axis=2), s_new)
    e = jnp.exp(s - mx[:, :, None])
    e_new = jnp.exp(s_new - mx)
    den = jnp.sum(e, axis=2) + e_new
    p = (e / den[:, :, None]).astype(jnp.bfloat16)
    p_new = (e_new / den).astype(jnp.bfloat16)
    o_all = jnp.einsum('bhl,blc->bhc', p, cache, preferred_element_type=jnp.float32)
    o_lat = (o_all[:, :, :kvl] + p_new.astype(jnp.float32)[:, :, None] * kv_new[:, None, :kvl].astype(jnp.float32)).astype(jnp.bfloat16)
    o = jnp.einsum('bhc,hcv->bhv', o_lat, w_uv, preferred_element_type=jnp.float32).astype(jnp.bfloat16).reshape(bsz, heads * vh)
    a = jnp.dot(o, w_o, preferred_element_type=jnp.float32)
    return (x.astype(jnp.float32) + a).astype(jnp.bfloat16), kv_new


def solution(mesh):
    n = mesh.shape['ep']
    tok_spec = P(('rep', 'ep'))
    row_spec = P(('rep', 'ep'), None)
    cache_spec = P(('rep', 'ep'), None, None)
    exp_spec = P('ep', None, None)

    def local(x, cache, lens, ids, rw, w_q, w_dkv, w_uk, w_uv, w_o, s_gate, s_up, s_down, e_gate, e_up, e_down):
        h1, kv_new = attention(x, cache, lens, w_q, w_dkv, w_uk, w_uv, w_o)
        u = rms(h1).astype(jnp.bfloat16)
        shared = swiglu(u, s_gate, s_up, s_down)
        b_dev, top = ids.shape
        hid = x.shape[1]
        e_loc = e_gate.shape[0]
        n_exp = e_loc * n
        cape = (CAP_FACTOR * b_dev * top + n_exp - 1) // n_exp
        disp, comb = route(ids, rw, n_exp, cape)
        send = jnp.einsum('br,bh->rh', disp, u, preferred_element_type=jnp.float32).astype(jnp.bfloat16)
        recv = lax.all_to_all(send, 'ep', 0, 0, tiled=True)
        xr = recv.reshape(n, e_loc, cape, hid).transpose(1, 0, 2, 3).reshape(e_loc, n * cape, hid)
        g = jnp.einsum('erh,ehi->eri', xr, e_gate, preferred_element_type=jnp.float32)
        v = jnp.einsum('erh,ehi->eri', xr, e_up, preferred_element_type=jnp.float32)
        act = (jax.nn.silu(g) * v).astype(jnp.bfloat16)
        out = jnp.einsum('eri,eih->erh', act, e_down, preferred_element_type=jnp.float32).astype(jnp.bfloat16)
        back = out.reshape(e_loc, n, cape, hid).transpose(1, 0, 2, 3).reshape(n_exp * cape, hid)
        ret = lax.all_to_all(back, 'ep', 0, 0, tiled=True)
        routed = jnp.dot(comb, ret, preferred_element_type=jnp.float32).reshape(-1, b_dev, hid).sum(axis=0)
        y = (h1.astype(jnp.float32) + shared + routed).astype(jnp.bfloat16)
        return y, kv_new

    in_specs = (row_spec, cache_spec, tok_spec, row_spec, row_spec) + (P(),) * 8 + (exp_spec,) * 3
    return jax.shard_map(local, mesh=mesh, in_specs=in_specs, out_specs=(row_spec, row_spec), check_vma=False)
```

profile of v0, /device:TPU:0, one launch (start us, length us, event | category | flops | bytes accessed | tf_op | source)
XLA Modules:
  0.0 258.8 jit_solution(8482858689549362956)
XLA Ops:
  0.7 1.3 fusion.22
  2.0 7.1 %convolution_convert_fusion = bf16[64,3072]{1,0:T(8,128)(2,1)S(1)} fusion(bf16[2048,3072]{1,0:T(8,128)(2,1)} %param.21, bf16[64,2048]{1,0:T(8,128)(2,1)} %param.16, f32[64]{0:T(128)S(1)} %add_rsqrt_fusion.2), kind=kOutput, calls=%fused_computation.5 | convolution fusion | flops 805896192 | bytes 13238528 | tf_op jit(solution)/shard_map/dot_general | solution.py:60
  9.0 0.6 reshape.166
  9.8 0.1 iota_compare_fusion.8
  9.9 0.8 fusion.42
  10.7 0.1 copy_convert_fusion
  10.8 0.1 multiply_reduce_fusion.1
  10.9 0.1 fusion.55
  11.0 0.2 subtract_convert_fusion.1
  11.2 0.0 copy-done.3
  11.2 0.4 fusion.12
  11.7 0.3 subtract_convert_fusion
  11.9 0.2 pad_maximum_fusion
  12.2 0.1 fusion.72
  12.3 0.9 fusion.16
  13.2 8.6 %fusion.56 = (f32[64,16]{1,0:T(8,128)S(1)}, f32[64,16,256]{2,1,0:T(8,128)S(1)}) fusion(bf16[64,256,576]{1,2,0:T(8,128)(2,1)} %param.17, bf16[64,16,576]{2,0,1:T(8,128)(2,1)S(1)} %pad_maximum_fusion, pred[64,256]{1,0:T(8,128)(4,1)S(1)} %iota_compare_fusion.8), kind=kOutput, calls=%fused_computation.97 | convolution fusion | flops 302775296 | bytes 21123072 | tf_op jit(solution)/shard_map/bhc,blc->bhl/dot_general | solution.py:67
  21.8 0.4 fusion.21
  22.1 8.1 %add_convert_fusion = bf16[64,16,512]{2,1,0:T(8,128)(2,1)S(1)} fusion(bf16[64,256,576]{1,2,0:T(8,128)(2,1)} %param.17, f32[64,512]{1,0:T(8,128)S(1)} %get-tuple-element.2, f32[64,16]{1,0:T(8,128)S(1)} %get-tuple-element.9, f32[64,16,256]{2,1,0:T(8,128)S(1)} %get-tuple-element.16, f32[64,16]{1,0:T(8,128)S(1)} %get-tuple-element.8, ...), kind=kOutput, calls=%fused_computation.17 | convolution fusion | flops 270794752 | bytes 19017728 | tf_op jit(solution)/shard_map/bhl,blc->bhc/dot_general | solution.py:77
  30.2 2.9 %fusion.15 = bf16[16,8,8,128]{3,2,1,0:T(8,128)(2,1)S(1)} fusion(bf16[16,512,128]{2,1,0:T(8,128)(2,1)} %param.24, bf16[64,16,512]{2,1,0:T(8,128)(2,1)S(1)} %add_convert_fusion), kind=kOutput, calls=%fused_computation.28 | convolution fusion | flops 134348800 | bytes 3407872 | tf_op jit(solution)/shard_map/bhc,hcv->bhv/dot_general | solution.py:79
  33.2 5.1 %multiply_reduce_fusion = (f32[64]{0:T(128)S(1)}, f32[64,2048]{1,0:T(8,128)S(1)}) fusion(bf16[2048,2048]{1,0:T(8,128)(2,1)} %param.25, bf16[16,8,8,128]{3,2,1,0:T(8,128)(2,1)S(1)} %fusion.15, bf16[64,2048]{1,0:T(8,128)(2,1)S(1)} %copy-done.2), kind=kOutput, calls=%fused_computation.44 | convolution fusion | flops 537657280 | bytes 9437440 | tf_op jit(solution)/shard_map/dot_general | solution.py:80
  38.3 0.1 copy.47
  38.4 0.1 eq.40
  38.5 0.2 fusion.19
  38.8 0.1 convert_element_type.143
  38.9 0.5 convolution_convert_fusion.5
  39.4 0.4 copy.51
  39.8 0.1 reshape.168
  39.9 1.0 convolution_convert_fusion.1
  41.0 41.5 %all_to_all.21 = bf16[4,192,2048]{2,1,0:T(8,128)(2,1)S(1)} all-to-all(bf16[4,192,2048]{2,1,0:T(8,128)(2,1)S(1)} %bitcast.65), channel_id=1, replica_groups=mesh['rep'=4,'ep'=4] {'ep'}, dimensions={0} | all-to-all | bytes 6291456 | tf_op jit(solution)/shard_map/all_to_all | solution.py:102
  82.5 2.4 copy.52
  84.9 3.4 %copy.53 = bf16[16,4,12,2048]{3,0,2,1:T(8,128)(2,1)} copy(bf16[16,4,12,2048]{3,1,2,0:T(4,128)(2,1)S(1)} %bitcast.66) | data formatting | bytes 6291456 | tf_op jit(solution)/shard_map/transpose | solution.py:103
  88.3 34.7 %fusion.4 = f32[16,48,1408]{2,1,0:T(8,128)} fusion(bf16[16,2048,1408]{2,1,0:T(8,128)(2,1)} %param.29, bf16[16,48,2048]{2,0,1:T(8,128)(2,1)} %bitcast.63), kind=kOutput, calls=%fused_computation.9 | convolution fusion | flops 4429185024 | bytes 99745792 | tf_op jit(solution)/shard_map/erh,ehi->eri/dot_general | solution.py:104
  123.0 35.3 %multiply_convert_fusion.clone.4 = bf16[16,48,1408]{2,1,0:T(8,128)(2,1)S(1)} fusion(f32[16,48,1408]{2,1,0:T(8,128)} %fusion.4, bf16[16,2048,1408]{2,1,0:T(8,128)(2,1)} %param.30, bf16[16,48,2048]{2,0,1:T(8,128)(2,1)} %bitcast.64), kind=kOutput, calls=%fused_computation.2.clone.clone.clone.1 | convolution fusion | flops 4435673088 | bytes 101908480 | tf_op jit(solution)/shard_map/erh,ehi->eri/dot_general | solution.py:105
  158.3 33.6 %convolution_convert_fusion.2 = bf16[16,48,2048]{2,1,0:T(8,128)(2,1)} fusion(bf16[16,1408,2048]{2,1,0:T(8,128)(2,1)} %param.31, bf16[16,48,1408]{2,1,0:T(8,128)(2,1)S(1)} %multiply_convert_fusion.clone.4), kind=kOutput, calls=%fused_computation.7 | convolution fusion | flops 4430757888 | bytes 97583104 | tf_op jit(solution)/shard_map/eri,eih->erh/dot_general | solution.py:107
  191.9 3.6 %copy.56 = bf16[16,48,2048]{2,0,1:T(8,128)(2,1)S(1)} copy(bf16[16,48,2048]{2,1,0:T(8,128)(2,1)} %convolution_convert_fusion.2) | data formatting | bytes 6291456 | tf_op jit(solution)/shard_map/convert_element_type | solution.py:107
  195.5 2.4 copy.57
  197.9 3.4 %copy.58 = bf16[4,192,2048]{2,1,0:T(8,128)(2,1)} copy(bf16[4,192,2048]{2,0,1:T(4,128)(2,1)S(1)} %bitcast.68) | data formatting | bytes 6291456 | tf_op jit(solution)/shard_map/all_to_all | solution.py:109
  201.4 5.0 %all-to-all-start.1 = ((bf16[4,192,2048]{2,1,0:T(8,128)(2,1)}), bf16[4,192,2048]{2,1,0:T(8,128)(2,1)}, u32[]{:S(2)}, u32[]{:S(2)}) async-start(bf16[4,192,2048]{2,1,0:T(8,128)(2,1)} %copy.58), calls=%async_computation.1 | async-start | bytes 6291456 | tf_op jit(solution)/shard_map/all_to_all | solution.py:109
  206.4 0.1 copy.48
  206.5 0.1 fusion.31
  206.7 0.9 fusion.14
  207.5 1.1 copy.50
  208.6 0.3 dot_general.72
  208.9 0.7 pad_maximum_fusion.1
  209.6 7.3 %fusion.54 = f32[64,2816]{1,0:T(8,128)} fusion(bf16[2048,2816]{1,0:T(8,128)(2,1)} %param.26, f32[64,2048]{1,0:T(8,128)S(1)} %get-tuple-element.18, f32[64]{0:T(128)S(1)} %add_rsqrt_fusion), kind=kOutput, calls=%fused_computation.95 | convolution fusion | flops 738459648 | bytes 12779776 | tf_op jit(solution)/shard_map/dot_general | solution.py:28
  216.9 26.1 %all-to-all-done.1 = bf16[4,192,2048]{2,1,0:T(8,128)(2,1)} async-done(((bf16[4,192,2048]{2,1,0:T(8,128)(2,1)}), bf16[4,192,2048]{2,1,0:T(8,128)(2,1)}, u32[]{:S(2)}, u32[]{:S(2)}) %all-to-all-start.1) | async-done | bytes 3145760 | tf_op jit(solution)/shard_map/all_to_all | solution.py:109
  243.0 2.7 %convolution_reduce_fusion = f32[64,2048]{1,0:T(8,128)S(1)} fusion(bf16[3,64,768]{1,2,0:T(8,128)(2,1)S(1)} %dot_general.72, bf16[768,2048,1]{1,0,2:T(8,128)(2,1)} %bitcast.19), kind=kOutput, calls=%fused_computation.22 | convolution fusion | flops 604241920 | bytes 3964928 | tf_op jit(solution)/shard_map/dot_general | solution.py:110
  245.7 12.9 %fusion.9 = bf16[64,2048]{1,0:T(8,128)(2,1)} fusion(f32[64,2048]{1,0:T(8,128)S(1)} %convolution_reduce_fusion, f32[64,2048]{1,0:T(8,128)S(1)} %get-tuple-element.18, bf16[2816,2048]{1,0:T(8,128)(2,1)} %param.28, bf16[2048,2816]{1,0:T(8,128)(2,1)} %param.27, f32[64,2816]{1,0:T(8,128)} %fusion.54, f32[64]{0:T(128)S(1)} %add_rsqrt_fusion), kind=kOutput, calls=%fused_computation.16 | convolution fusion | flops 1478131712 | bytes 25100544 | tf_op jit(solution)/shard_map/dot_general | solution.py:30
  (25 shorter events, 0.2 us)
Async XLA Ops:
  0.6 9.2 %copy-start = (bf16[2048,576]{0,1:T(8,128)(2,1)S(1)}, bf16[2048,576]{0,1:T(8,128)(2,1)}, u32[]{:S(2)}) copy-start(bf16[2048,576]{0,1:T(8,128)(2,1)} %param.22) | copy-start | bytes 7077892
  1.9 7.8 %copy-start.6 = (s32[64]{0:T(128)S(1)}, s32[64]{0:T(128)}, u32[]{:S(2)}) copy-start(s32[64]{0:T(128)} %param.18) | copy-start | bytes 772
  1.9 7.9 %copy-start.2 = (bf16[64,2048]{1,0:T(8,128)(2,1)S(1)}, bf16[64,2048]{1,0:T(8,128)(2,1)}, u32[]{:S(2)}) copy-start(bf16[64,2048]{1,0:T(8,128)(2,1)} %param.16) | copy-start | bytes 786436
  9.6 1.6 copy-start.3
  33.2 5.1 %copy-start.4 = (s32[64,6]{0,1:T(8,128)S(1)}, s32[64,6]{0,1:T(8,128)}, u32[]{:S(2)}) copy-start(s32[64,6]{0,1:T(8,128)} %param.19) | copy-start | bytes 4612
  201.4 5.0 %copy-start.5 = (f32[64,6]{0,1:T(8,128)S(1)}, f32[64,6]{0,1:T(8,128)}, u32[]{:S(2)}) copy-start(f32[64,6]{0,1:T(8,128)} %param.20) | copy-start | bytes 4612
  201.4 41.6 %all-to-all-start.1 = ((bf16[4,192,2048]{2,1,0:T(8,128)(2,1)}), bf16[4,192,2048]{2,1,0:T(8,128)(2,1)}, u32[]{:S(2)}, u32[]{:S(2)}) async-start(bf16[4,192,2048]{2,1,0:T(8,128)(2,1)} %copy.58), calls=%async_computation.1 | async-start | bytes 6291456 | tf_op jit(solution)/shard_map/all_to_all | solution.py:109
  245.7 12.9 %copy-start.1 = (bf16[2048,576]{0,1:T(8,128)(2,1)S(1)}, bf16[2048,576]{0,1:T(8,128)(2,1)}, u32[]{:S(2)}) copy-start(bf16[2048,576]{0,1:T(8,128)(2,1)} %param.22) | copy-start | bytes 7077892
where the time goes:
time: 263 us; the launch traced here: 259 us
  matrix products  163 us (62%)
  blocking collectives  41.5 us (16%)
  waiting for transfers between devices  26.1 us (10%)
  local copies, waits for them, and re-layouts  18.4 us (7%)
  starting transfers between devices  4.98 us (2%)
  other arithmetic  3.66 us (1%)
    all_to_all x1, blocking collectives, local(): recv = lax.all_to_all(send, 'ep', 0, 0, tiled=True)  41.5 us
    dot_general x1, matrix products, local(): v = jnp.einsum('erh,ehi->eri', xr, e_up, preferred_element_type=jnp.float32)  35.3 us
    dot_general x1, matrix products, local(): jnp.einsum('erh,ehi->eri', xr, e_gate, preferred_element_type=jnp.float32)  34.7 us
    dot_general x1, matrix products, local(): jnp.einsum('eri,eih->erh', act, e_down, preferred_element_type=jnp.float32)  33.6 us
    all_to_all x1, waiting for transfers between devices, local(): ret = lax.all_to_all(back, 'ep', 0, 0, tiled=True)  26.1 us
    dot_general x1, matrix products, swiglu(): jnp.dot((jax.nn.silu(g) * v).astype(jnp.bfloat16), wd, preferred_element_...  12.9 us
    dot_general x1, matrix products, attention(): jnp.einsum('bhc,blc->bhl', qf, cache, preferred_element_type=jnp.float32)  8.56 us
    dot_general x1, matrix products, attention(): jnp.einsum('bhl,blc->bhc', p, cache, preferred_element_type=jnp.float32)  8.09 us
  transfers between devices with their start and end apart: 1, of which 1 were waited for; matrix products, arithmetic and copies ran while one was open for 4% of the time, Pallas kernels for 0%

commit v1 on v0

v1 whole, which is shorter than its diff:
```python
import math

import numpy as np
import jax
import jax.numpy as jnp
from jax import lax
from jax.experimental import pallas as pl
from jax.experimental.pallas import tpu as pltpu
from jax.sharding import PartitionSpec as P

EPS = 1e-6
ROPE_BASE = 1.0e4
CAP_FACTOR = 2
F32 = jnp.float32
BF16 = jnp.bfloat16
NSLOT = 5
NCACHE = 6
GROUP = 8
NCHUNK = 4
MESH = pl.DeviceIdType.MESH


def dot(a, b):
    return jnp.dot(a, b, preferred_element_type=F32)


def dot_nt(a, b):
    return lax.dot_general(a, b, (((1,), (1,)), ((), ())), preferred_element_type=F32)


def rms(v):
    return v * lax.rsqrt(jnp.mean(v * v, axis=-1, keepdims=True) + EPS)


def silu(g):
    return g / (1.0 + jnp.exp(-g))


def tiles(width, step):
    return [(a, min(step, width - a)) for a in range(0, width, step)]


def iota(shape, dim):
    return lax.broadcasted_iota(jnp.int32, shape, dim)


def layer_kernel(cape, lens_s, lens_v, inv, x, ids, rw, cache, w_q, w_dkv, w_uk, w_uv, w_o, s_gate, s_up, s_down, e_gate, e_up, e_down,
                 y, kvn,
                 ring, cbuf, dkv_b, uk_b, uv_b, q_s, qf, kv_s, o_s, h1_s, u_all, gw_all, d_s, w_s, xr, acts, acts_sh, outs, rp, xs, rc, sh,
                 ring_sem, c_sem, w_sem, gw_send, gw_recv, u_send, u_recv, p_send, p_recv, x_send, x_recv):
    bsz, hid = x.shape
    heads, nope, kvl = w_uk.shape
    kvd = cache.shape[2]
    lmax = cache.shape[1]
    qkd = nope + kvd - kvl
    vh = w_uv.shape[2]
    n_loc = e_gate.shape[0]
    inter = e_gate.shape[2]
    n_dev = gw_all.shape[0] // bsz
    rows_e = n_dev * cape
    cw = hid // NCHUNK
    grows = GROUP * heads
    nlat = kvl // 128
    cb = cw // 128
    me = lax.axis_index("ep")

    def peer(k):
        return jnp.bitwise_xor(me, k)

    barrier = pltpu.get_barrier_semaphore()
    for k in range(1, n_dev):
        pl.semaphore_signal(barrier, inc=1, device_id={"ep": peer(k)}, device_id_type=MESH)

    def to_slot(src, slot, rows=None, cols=None):
        dst = ring.at[slot]
        if rows is not None:
            dst = ring.at[slot, pl.ds(0, rows), pl.ds(0, cols)]
        return pltpu.make_async_copy(src, dst, ring_sem.at[slot])

    def wq_job(i):
        a = i * inter
        w = min(inter, w_q.shape[1] - a)
        return to_slot(w_q.at[:, pl.ds(a, w)], i, hid, w)

    def wo_job(i):
        a = i * inter
        w = min(inter, hid - a)
        return to_slot(w_o.at[:, pl.ds(a, w)], 3 + i, heads * vh, w)

    def sgu_job(i):
        src = s_gate if i % 2 == 0 else s_up
        return to_slot(src.at[:, pl.ds((i // 2) * inter, inter)], (5 + i) % NSLOT)

    def gate_job(e):
        return to_slot(e_gate.at[e], lax.rem(9 + 2 * e, NSLOT))

    def up_job(e):
        return to_slot(e_up.at[e], lax.rem(10 + 2 * e, NSLOT))

    def down_job(i):
        e = lax.rem(i, n_loc)
        c = pl.multiple_of((i // n_loc) * cw, cw)
        return to_slot(e_down.at[e, :, pl.ds(c, cw)], lax.rem(41 + i, NSLOT), inter, cw)

    def sd_job(i):
        r = i % 2
        c = i // 2
        half = hid // 2
        return to_slot(s_down.at[pl.ds(r * inter, inter), pl.ds(c * half, half)], (105 + i) % NSLOT, inter, half)

    def cache_job(g):
        s = lax.rem(g, NCACHE)
        return pltpu.make_async_copy(cache.at[pl.ds(g * GROUP, GROUP)], cbuf.at[s], c_sem.at[s])

    dkv_copy = pltpu.make_async_copy(w_dkv, dkv_b, w_sem.at[0])
    uk_copy = pltpu.make_async_copy(w_uk, uk_b, w_sem.at[1])
    uv_copy = pltpu.make_async_copy(w_uv, uv_b, w_sem.at[2])
    for i in range(3):
        wq_job(i).start()
    dkv_copy.start()
    uk_copy.start()
    for g in range(NCACHE):
        cache_job(g).start()
    uv_copy.start()
    for i in range(2):
        wo_job(i).start()

    col = iota((bsz, 128), 1)
    gw = jnp.zeros((bsz, 128), F32)
    for k in range(ids.shape[1]):
        gw = gw + jnp.where(ids[:, k:k + 1] == col, rw[:, k:k + 1], 0.0)
    gw_all[pl.ds(pl.multiple_of(me * bsz, bsz), bsz), :] = gw

    diag = iota((bsz, bsz), 0) == iota((bsz, bsz), 1)
    pos = jnp.sum(jnp.where(diag, jnp.broadcast_to(lens_v[...], (bsz, bsz)), 0), axis=1, keepdims=True).astype(F32)
    ang = pos * inv[...]
    cs = jnp.cos(ang)
    half = (kvd - kvl) // 2
    low = col < half
    sn = jnp.where(low, -1.0, 1.0) * jnp.sin(ang)

    def rope(v):
        sw = jnp.where(low, pltpu.roll(v, 128 - half, 1), pltpu.roll(v, half, 1))
        return v * cs + sw * sn

    xf = x[...].astype(F32)
    xn = rms(xf).astype(BF16)

    pl.semaphore_wait(barrier, n_dev - 1)

    def gw_copy(k):
        mine = gw_all.at[pl.ds(pl.multiple_of(me * bsz, bsz), bsz)]
        return pltpu.make_async_remote_copy(mine, mine, gw_send.at[k - 1], gw_recv.at[k - 1], device_id={"ep": peer(k)}, device_id_type=MESH)

    for k in range(1, n_dev):
        gw_copy(k).start()

    for i in range(3):
        wq_job(i).wait()
        a = i * inter
        for b, w in tiles(min(inter, w_q.shape[1] - a), 512):
            q_s[:, a + b:a + b + w] = dot(xn, ring[i, :, b:b + w]).astype(BF16)
    dkv_copy.wait()
    kv = dot(xn, dkv_b[...])
    kv_s[...] = jnp.zeros_like(kv_s)
    kv_s[:, :kvd] = kv
    kvn[:, :kvl] = rms(kv_s[:, :kvl]).astype(BF16)
    kvn[:, kvl:] = rope(kv_s[:, kvl:kvl + 128])[:, :kvd - kvl].astype(BF16)

    uk_copy.wait()
    left = col < 64

    def put_head(h, q_nope, q_rot):
        ql = dot(q_nope.astype(BF16), uk_b[h])
        for c in range(nlat):
            qf[c, pl.ds(h, bsz, stride=heads), :] = ql[:, 128 * c:128 * (c + 1)]
        qf[nlat, pl.ds(h, bsz, stride=heads), :] = jnp.where(left, rope(q_rot), 0.0)

    for hp in range(heads // 2):
        a = hp * 2 * qkd
        b0 = q_s[:, a:a + 128].astype(F32)
        b1 = q_s[:, a + 128:a + 256].astype(F32)
        b2 = q_s[:, a + 256:a + 384].astype(F32)
        r1 = pltpu.roll(b1, 64, 1)
        r2 = pltpu.roll(b2, 64, 1)
        put_head(2 * hp, b0, b1)
        put_head(2 * hp + 1, jnp.where(left, r1, r2), r2)

    scale = qkd ** -0.5
    tpos = iota((heads, lmax), 1)
    seq_of_row = iota((grows, bsz), 0) // heads
    seq_col = iota((grows, bsz), 1)

    def attend(g, carry):
        s = lax.rem(g, NCACHE)
        cache_job(g).wait()
        rows = pl.ds(pl.multiple_of(g * grows, grows), grows)
        qg = jnp.concatenate([qf[c, rows, :].astype(BF16) for c in range(nlat + 1)], axis=1)[:, :kvd]
        own = seq_col == seq_of_row + g * GROUP
        s_new = jnp.sum(jnp.where(own, dot_nt(qg, kvn[...]), 0.0), axis=1, keepdims=True) * scale
        parts = []
        for i in range(GROUP):
            si = dot_nt(qg[i * heads:(i + 1) * heads], cbuf[s, i]) * scale
            parts.append(jnp.where(tpos < lens_s[g * GROUP + i], si, -jnp.inf))
        sc = jnp.concatenate(parts, axis=0)
        mx = jnp.maximum(jnp.max(sc, axis=1, keepdims=True), s_new)
        e = jnp.exp(sc - mx)
        e_new = jnp.exp(s_new - mx)
        den = jnp.sum(e, axis=1, keepdims=True) + e_new
        rden = 1.0 / den
        p = (e * rden).astype(BF16)
        p_new = jnp.where(own, e_new * rden, 0.0).astype(BF16)
        o_new = dot(p_new, kvn[:, :kvl])
        outs_i = [dot(p[i * heads:(i + 1) * heads], cbuf[s, i, :, :kvl]) for i in range(GROUP)]
        o_lat = jnp.concatenate(outs_i, axis=0) + o_new
        for c in range(nlat):
            qf[c, rows, :] = o_lat[:, 128 * c:128 * (c + 1)]

        @pl.when(g + NCACHE < bsz // GROUP)
        def _():
            cache_job(g + NCACHE).start()

        @pl.when(g == bsz // GROUP - NCACHE - 1)
        def _():
            for i in range(3):
                sgu_job(i).start()
        return carry

    lax.fori_loop(0, bsz // GROUP, attend, 0)

    uv_copy.wait()
    for h in range(heads):
        oh = jnp.concatenate([qf[c, pl.ds(h, bsz, stride=heads), :].astype(BF16) for c in range(nlat)], axis=1)
        o_s[:, h * vh:(h + 1) * vh] = dot(oh, uv_b[h]).astype(BF16)
    for i in range(2):
        wo_job(i).wait()
        a = i * inter
        for b, w in tiles(min(inter, hid - a), 512):
            h1_s[:, a + b:a + b + w] = (x[:, a + b:a + b + w].astype(F32) + dot(o_s[...], ring[3 + i, :, b:b + w])).astype(BF16)
    sgu_job(3).start()
    gate_job(0).start()

    u = rms(h1_s[...].astype(F32)).astype(BF16)
    mine = pl.ds(pl.multiple_of(me * bsz, bsz), bsz)
    across = pl.ds(pl.multiple_of(peer(2) * bsz, bsz), bsz)
    u_all[mine, :] = u

    def u_copy(rows, i, k):
        blk = u_all.at[rows]
        return pltpu.make_async_remote_copy(blk, blk, u_send.at[i], u_recv.at[i], device_id={"ep": peer(k)}, device_id_type=MESH)

    u_copy(mine, 1, 2).start()
    u_copy(mine, 0, 1).start()

    def shared_gu(i):
        for j in range(2):
            sgu_job(2 * i + j).wait()
        uu = u_all[mine, :]
        for b, w in tiles(inter, 512):
            gg = dot(uu, ring[(5 + 2 * i) % NSLOT, :, b:b + w])
            vv = dot(uu, ring[(6 + 2 * i) % NSLOT, :, b:b + w])
            acts_sh[:, i * inter + b:i * inter + b + w] = (silu(gg) * vv).astype(BF16)

    shared_gu(0)
    up_job(0).start()
    gate_job(1).start()
    shared_gu(1)
    up_job(1).start()
    gate_job(2).start()

    for k in range(1, n_dev):
        gw_copy(k).wait()
    nt = n_dev * bsz
    ga = gw_all[...]
    hit = ga > 0.0
    ti = iota((nt, nt), 0)
    tj = iota((nt, nt), 1)
    before = ((ti // bsz == tj // bsz) & (tj < ti)).astype(F32).astype(BF16)
    rank = dot(before, jnp.where(hit, 1.0, 0.0).astype(BF16))
    src = (iota((nt, 128), 0) // bsz * cape).astype(F32)
    code = jnp.where(hit, src + rank, -1.0)
    exp_r = iota((128, n_loc * rows_e), 0)
    exp_c = iota((128, n_loc * rows_e), 1) // rows_e
    spread = (exp_r == exp_c + me * n_loc).astype(F32).astype(BF16)
    code_x = dot(code.astype(BF16), spread)
    slot_c = (iota((nt, n_loc * rows_e), 1) % rows_e).astype(F32)
    member = code_x == slot_c
    g1 = ga.astype(BF16)
    res = ga - g1.astype(F32)
    g2 = res.astype(BF16)
    g3 = (res - g2.astype(F32)).astype(BF16)
    for t, gt in enumerate((g1, g2, g3)):
        w_s[t] = jnp.where(member, dot(gt, spread), 0.0).astype(BF16)
    d_s[...] = jnp.where(member, 1.0, 0.0).T.astype(BF16)

    u_copy(mine, 1, 2).wait_recv()
    u_copy(across, 2, 1).start()
    u_copy(mine, 0, 1).wait()
    u_copy(across, 2, 1).wait()
    u_copy(mine, 1, 2).wait_send()

    def gate_up(e, carry):
        erows = pl.ds(pl.multiple_of(e * rows_e, rows_e), rows_e)
        de = d_s[erows, :]
        for b, w in tiles(hid, 512):
            xr[:, b:b + w] = dot(de, u_all[:, b:b + w]).astype(BF16)
        gate_job(e).wait()
        up_job(e).wait()
        sg = lax.rem(9 + 2 * e, NSLOT)
        su = lax.rem(10 + 2 * e, NSLOT)
        for b, w in tiles(inter, 512):
            gg = dot(xr[...], ring[sg, :, b:b + w])
            vv = dot(xr[...], ring[su, :, b:b + w])
            acts[erows, b:b + w] = (silu(gg) * vv).astype(BF16)

        @pl.when(e + 2 < n_loc)
        def _():
            up_job(e + 2).start()

        @pl.when(e + 2 >= n_loc)
        def _():
            down_job(14 + 2 * e - 41).start()

        @pl.when(e + 3 < n_loc)
        def _():
            gate_job(e + 3).start()

        @pl.when(e + 3 >= n_loc)
        def _():
            down_job(15 + 2 * e - 41).start()
        return carry

    lax.fori_loop(0, n_loc, gate_up, 0)

    def part(j, d):
        return pl.ds(pl.multiple_of(j * nt + d * bsz, bsz), bsz)

    def pair_copy(j, i, d):
        return pltpu.make_async_remote_copy(qf.at[pl.ds(0, cb), part(j, d)], rp.at[i, pl.ds(j * cb, cb)],
                                            p_send.at[j, i], p_recv.at[j, i], device_id={"ep": peer(1)}, device_id_type=MESH)

    def cross_copy(j):
        blk = pl.ds(j * cb, cb)
        return pltpu.make_async_remote_copy(xs.at[blk], rc.at[blk], x_send.at[j], x_recv.at[j],
                                            device_id={"ep": peer(2)}, device_id_type=MESH)

    def start_pair(j):
        pair_copy(j, 1, peer(3)).start()
        pair_copy(j, 0, peer(1)).start()

    def forward(j):
        pair_copy(j, 1, peer(3)).wait_recv()
        for c in range(cb):
            xs[j * cb + c] = qf[c, part(j, peer(2)), :] + rp[1, j * cb + c]
        cross_copy(j).start()

    for j in range(NCHUNK):
        def down(e, carry):
            i = j * n_loc + e
            down_job(i).wait()
            erows = pl.ds(pl.multiple_of(e * rows_e, rows_e), rows_e)
            outs[erows, :] = dot(acts[erows, :], ring[lax.rem(41 + i, NSLOT), :inter, :cw]).astype(BF16)
            if j < NCHUNK - 1:
                down_job(i + NSLOT).start()
            else:
                @pl.when(e + NSLOT < n_loc)
                def _():
                    down_job(i + NSLOT).start()
                for k in range(4):
                    @pl.when(e == n_loc - NSLOT + k)
                    def _():
                        sd_job(k).start()
            return carry

        lax.fori_loop(0, n_loc, down, 0)
        if j >= 1:
            forward(j - 1)
        ov = outs[...]
        total = dot(w_s[0], ov) + dot(w_s[1], ov) + dot(w_s[2], ov)
        for c in range(cb):
            qf[c, pl.ds(j * nt, nt), :] = total[:, 128 * c:128 * (c + 1)]
        start_pair(j)

    hw = hid // 2
    for c in range(2):
        for r in range(2):
            sd_job(2 * c + r).wait()
        for b, w in tiles(hw, 512):
            acc = dot(acts_sh[:, :inter], ring[(105 + 2 * c) % NSLOT, :inter, b:b + w])
            acc += dot(acts_sh[:, inter:], ring[(106 + 2 * c) % NSLOT, :inter, b:b + w])
            sh[:, c * hw + b:c * hw + b + w] = acc
        if c == 0:
            forward(NCHUNK - 1)

    for j in range(NCHUNK):
        pair_copy(j, 0, peer(1)).wait_recv()
        cross_copy(j).wait_recv()
        for c in range(cb):
            b = j * cb + c
            cols = slice(b * 128, (b + 1) * 128)
            routed = qf[c, part(j, me), :] + rp[0, b] + rc[b]
            y[:, cols] = (h1_s[:, cols].astype(F32) + sh[:, cols] + routed).astype(BF16)
    for j in range(NCHUNK):
        pair_copy(j, 1, peer(3)).wait_send()
        pair_copy(j, 0, peer(1)).wait_send()
        cross_copy(j).wait_send()


def solution(mesh):
    n = mesh.shape['ep']
    tok_spec = P(('rep', 'ep'))
    row_spec = P(('rep', 'ep'), None)
    cache_spec = P(('rep', 'ep'), None, None)
    exp_spec = P('ep', None, None)

    def local(x, cache, lens, ids, rw, w_q, w_dkv, w_uk, w_uv, w_o, s_gate, s_up, s_down, e_gate, e_up, e_down):
        bsz, hid = x.shape
        heads, nope, kvl = w_uk.shape
        lmax, kvd = cache.shape[1:]
        n_loc, _, inter = e_gate.shape
        top = ids.shape[1]
        n_exp = n_loc * n
        cape = (CAP_FACTOR * bsz * top + n_exp - 1) // n_exp
        rows_e = n * cape
        nt = n * bsz
        cw = hid // NCHUNK
        half = (kvd - kvl) // 2
        inv = np.float64(ROPE_BASE) ** (-2.0 * (np.arange(128) % half) / (kvd - kvl))
        inv = jnp.asarray(inv.astype(np.float32)[None, :])
        vm = pl.BlockSpec(memory_space=pltpu.VMEM)
        hb = pl.BlockSpec(memory_space=pl.ANY)
        dma = pltpu.SemaphoreType.DMA
        call = pl.pallas_call(
            lambda *refs: layer_kernel(cape, *refs),
            name="layer",
            out_shape=(jax.ShapeDtypeStruct((bsz, hid), BF16), jax.ShapeDtypeStruct((bsz, kvd), BF16)),
            in_specs=[pl.BlockSpec(memory_space=pltpu.SMEM)] + [vm] * 5 + [hb] * 12,
            out_specs=(vm, vm),
            scratch_shapes=[
                pltpu.VMEM((NSLOT, hid, inter), BF16),
                pltpu.VMEM((NCACHE, GROUP, lmax, kvd), BF16),
                pltpu.VMEM(w_dkv.shape, BF16),
                pltpu.VMEM(w_uk.shape, BF16),
                pltpu.VMEM(w_uv.shape, BF16),
                pltpu.VMEM((bsz, w_q.shape[1]), BF16),
                pltpu.VMEM((kvl // 128 + 1, bsz * heads, 128), F32),
                pltpu.VMEM((bsz, kvl + 128), F32),
                pltpu.VMEM((bsz, hid), BF16),
                pltpu.VMEM((bsz, hid), BF16),
                pltpu.VMEM((nt, hid), BF16),
                pltpu.VMEM((nt, 128), F32),
                pltpu.VMEM((n_loc * rows_e, nt), BF16),
                pltpu.VMEM((3, nt, n_loc * rows_e), BF16),
                pltpu.VMEM((rows_e, hid), BF16),
                pltpu.VMEM((n_loc * rows_e, inter), BF16),
                pltpu.VMEM((bsz, 2 * inter), BF16),
                pltpu.VMEM((n_loc * rows_e, cw), BF16),
                pltpu.VMEM((2, hid // 128, bsz, 128), F32),
                pltpu.VMEM((hid // 128, bsz, 128), F32),
                pltpu.VMEM((hid // 128, bsz, 128), F32),
                pltpu.VMEM((bsz, hid), F32),
                dma((NSLOT,)), dma((NCACHE,)), dma((3,)),
                dma((n - 1,)), dma((n - 1,)), dma((3,)), dma((3,)),
                dma((NCHUNK, 2)), dma((NCHUNK, 2)), dma((NCHUNK,)), dma((NCHUNK,)),
            ],
            compiler_params=pltpu.CompilerParams(collective_id=0, has_side_effects=True, vmem_limit_bytes=67_043_328),
        )
        return call(lens, lens.reshape(1, bsz), inv, x, ids, rw, cache, w_q, w_dkv, w_uk, w_uv, w_o, s_gate, s_up, s_down, e_gate, e_up, e_down)

    in_specs = (row_spec, cache_spec, tok_spec, row_spec, row_spec) + (P(),) * 8 + (exp_spec,) * 3
    return jax.shard_map(local, mesh=mesh, in_specs=in_specs, out_specs=(row_spec, row_spec), check_vma=False)
```

time: 263 us -> 162 us (0.62); the launches traced: 259 us -> 161 us
  matrix products: 163 us -> 0 us
  Pallas kernels: 0 us -> 123 us
  blocking collectives: 41.5 us -> 0 us
  waiting for transfers between devices: 26.1 us -> 0 us
  local copies, waits for them, and re-layouts: 18.4 us -> 37 us
  starting transfers between devices: 4.98 us -> 0 us
  other arithmetic: 3.66 us -> 0 us
    dot_general x18 -> x0, matrix products: 163 us -> none  [the longest x1 35.3 us: local(): v = jnp.einsum('erh,ehi->eri', xr, e_up, preferred_element_type=jnp.float32)]
    pallas_call x0 -> x1, Pallas kernels: none -> 123 us  [local(): call(lens, lens.reshape(1, bsz), inv, x, ids, rw, cache, w_q, w_dkv, w_uk...]
    all_to_all x1 -> x0, blocking collectives: 41.5 us -> none  [local(): recv = lax.all_to_all(send, 'ep', 0, 0, tiled=True)]
    unnamed x15 -> x6, local copies, waits for them, and re-layouts: 0.17 us -> 37 us
    all_to_all x1 -> x0, waiting for transfers between devices: 26.1 us -> none  [local(): ret = lax.all_to_all(back, 'ep', 0, 0, tiled=True)]
    all_to_all x2 -> x0, local copies, waits for them, and re-layouts: 5.85 us -> none  [the longest x1 3.43 us: local(): ret = lax.all_to_all(back, 'ep', 0, 0, tiled=True)]
    transpose x2 -> x0, local copies, waits for them, and re-layouts: 5.83 us -> none  [the longest x1 3.4 us: local(): recv.reshape(n, e_loc, cape, hid).transpose(1, 0, 2, 3)]
    convert_element_type x4 -> x0, local copies, waits for them, and re-layouts: 5.19 us -> none  [the longest x1 3.62 us: local(): jnp.einsum('eri,eih->erh', act, e_down, preferred_element_type=jnp.float32)]
  transfers between devices with their start and end apart: 1 -> 0, of which waited for: 1 -> 0; matrix products, arithmetic and copies ran while one was open for 4% -> 0% of each run, Pallas kernels for 0% -> 0%
where the time goes in v1:
time: 162 us; the launch traced here: 161 us
  Pallas kernels  123 us (76%)
  local copies, waits for them, and re-layouts  37 us (23%)
    pallas_call x1, Pallas kernels, local(): call(lens, lens.reshape(1, bsz), inv, x, ids, rw, cache, w_q, w_dkv, w_uk...  123 us
    unnamed x6, local copies, waits for them, and re-layouts  37 us

profile of v1, /device:TPU:0, one launch (start us, length us, event | category | flops | bytes accessed | tf_op | source)
XLA Modules:
  0.0 160.6 jit_solution(6906175101313371216)
XLA Ops:
  0.6 1.4 copy.19.refs_4_
  2.0 1.4 copy.20.refs_5_
  3.4 4.4 %copy.22.refs_8_ = bf16[2048,576]{1,0:T(8,128)(2,1)} copy(bf16[2048,576]{0,1:T(8,128)(2,1)} %param.23) | data formatting | bytes 4718592 | tf_op args[6]
  7.8 26.7 %copy.21.refs_6_ = bf16[64,256,576]{2,1,0:T(8,128)(2,1)} copy(bf16[64,256,576]{1,2,0:T(8,128)(2,1)} %param.18) | data formatting | bytes 37748736 | tf_op args[1]
  34.4 122.9 %layer.1 = (bf16[64,2048]{1,0:T(8,128)(2,1)}, bf16[64,576]{1,0:T(8,128)(2,1)}) custom-call(s32[64]{0:T(128)} %refs_0_.1, s32[1,64]{1,0:T(1,128)} %bitcast.1, f32[1,128]{1,0:T(1,128)} %constant.2.clone.refs_2_, bf16[64,2048]{1,0:T(8,128)(2,1)} %refs_3_.1, s32[64,6]{1,0:T(8,128)} %copy.19.refs_4_, f32[64,6]{1,0:T(8,128)} %copy.20.refs_5_, ...), custom_call_target="tpu_custom_call" | custom-call | tf_op jit(solution)/shard_map/layer/pallas_call | solution.py:468
  157.4 1.7 %copy.25 = bf16[64,2048]{1,0:T(8,128)(2,1)} copy(bf16[64,2048]{1,0:T(8,128)(2,1)} %get-tuple-element.4) | data formatting | bytes 524288
  159.1 1.5 copy.26

commit v2 on v1

--- a/solution.py
+++ b/solution.py
@@ -50,8 +50,7 @@
                  ring_sem, c_sem, w_sem, gw_send, gw_recv, u_send, u_recv, p_send, p_recv, x_send, x_recv):
     bsz, hid = x.shape
     heads, nope, kvl = w_uk.shape
-    kvd = cache.shape[2]
-    lmax = cache.shape[1]
+    kvd, lmax = cache.shape[1:]
     qkd = nope + kvd - kvl
     vh = w_uv.shape[2]
     n_loc = e_gate.shape[0]
@@ -126,10 +125,11 @@
         wo_job(i).start()
 
     col = iota((bsz, 128), 1)
-    gw = jnp.zeros((bsz, 128), F32)
-    for k in range(ids.shape[1]):
-        gw = gw + jnp.where(ids[:, k:k + 1] == col, rw[:, k:k + 1], 0.0)
-    gw_all[pl.ds(pl.multiple_of(me * bsz, bsz), bsz), :] = gw
+    expert = iota((128, bsz), 0)
+    gw = jnp.zeros((128, bsz), F32)
+    for k in range(ids.shape[0]):
+        gw = gw + jnp.where(ids[k:k + 1, :] == expert, rw[k:k + 1, :], 0.0)
+    gw_all[pl.ds(pl.multiple_of(me * bsz, bsz), bsz), :] = gw.T
 
     diag = iota((bsz, bsz), 0) == iota((bsz, bsz), 1)
     pos = jnp.sum(jnp.where(diag, jnp.broadcast_to(lens_v[...], (bsz, bsz)), 0), axis=1, keepdims=True).astype(F32)
@@ -161,7 +161,7 @@
         for b, w in tiles(min(inter, w_q.shape[1] - a), 512):
             q_s[:, a + b:a + b + w] = dot(xn, ring[i, :, b:b + w]).astype(BF16)
     dkv_copy.wait()
-    kv = dot(xn, dkv_b[...])
+    kv = dot_nt(xn, dkv_b[...])
     kv_s[...] = jnp.zeros_like(kv_s)
     kv_s[:, :kvd] = kv
     kvn[:, :kvl] = rms(kv_s[:, :kvl]).astype(BF16)
@@ -200,7 +200,7 @@
         s_new = jnp.sum(jnp.where(own, dot_nt(qg, kvn[...]), 0.0), axis=1, keepdims=True) * scale
         parts = []
         for i in range(GROUP):
-            si = dot_nt(qg[i * heads:(i + 1) * heads], cbuf[s, i]) * scale
+            si = dot(qg[i * heads:(i + 1) * heads], cbuf[s, i]) * scale
             parts.append(jnp.where(tpos < lens_s[g * GROUP + i], si, -jnp.inf))
         sc = jnp.concatenate(parts, axis=0)
         mx = jnp.maximum(jnp.max(sc, axis=1, keepdims=True), s_new)
@@ -211,7 +211,7 @@
         p = (e * rden).astype(BF16)
         p_new = jnp.where(own, e_new * rden, 0.0).astype(BF16)
         o_new = dot(p_new, kvn[:, :kvl])
-        outs_i = [dot(p[i * heads:(i + 1) * heads], cbuf[s, i, :, :kvl]) for i in range(GROUP)]
+        outs_i = [dot_nt(p[i * heads:(i + 1) * heads], cbuf[s, i, :kvl, :]) for i in range(GROUP)]
         o_lat = jnp.concatenate(outs_i, axis=0) + o_new
         for c in range(nlat):
             qf[c, rows, :] = o_lat[:, 128 * c:128 * (c + 1)]
@@ -438,8 +438,8 @@
             out_specs=(vm, vm),
             scratch_shapes=[
                 pltpu.VMEM((NSLOT, hid, inter), BF16),
-                pltpu.VMEM((NCACHE, GROUP, lmax, kvd), BF16),
-                pltpu.VMEM(w_dkv.shape, BF16),
+                pltpu.VMEM((NCACHE, GROUP, kvd, lmax), BF16),
+                pltpu.VMEM(w_dkv.shape[::-1], BF16),
                 pltpu.VMEM(w_uk.shape, BF16),
                 pltpu.VMEM(w_uv.shape, BF16),
                 pltpu.VMEM((bsz, w_q.shape[1]), BF16),
@@ -465,7 +465,8 @@
             ],
             compiler_params=pltpu.CompilerParams(collective_id=0, has_side_effects=True, vmem_limit_bytes=67_043_328),
         )
-        return call(lens, lens.reshape(1, bsz), inv, x, ids, rw, cache, w_q, w_dkv, w_uk, w_uv, w_o, s_gate, s_up, s_down, e_gate, e_up, e_down)
+        return call(lens, lens.reshape(1, bsz), inv, x, ids.T, rw.T, cache.transpose(0, 2, 1), w_q, w_dkv.T, w_uk, w_uv, w_o,
+                    s_gate, s_up, s_down, e_gate, e_up, e_down)
 
     in_specs = (row_spec, cache_spec, tok_spec, row_spec, row_spec) + (P(),) * 8 + (exp_spec,) * 3
     return jax.shard_map(local, mesh=mesh, in_specs=in_specs, out_specs=(row_spec, row_spec), check_vma=False)

time: 162 us -> 126 us (0.78)
  local copies, waits for them, and re-layouts: 37 us -> 3.2 us
    unnamed x6 -> x2, local copies, waits for them, and re-layouts: 37 us -> 3.2 us
where the time goes in v2:
time: 126 us
  Pallas kernels  122 us (97%)
  local copies, waits for them, and re-layouts  3.2 us (3%)
    pallas_call x1, Pallas kernels, local(): call(lens, lens.reshape(1, bsz), inv, x, ids.T, rw.T, cache.transpose(0,...  122 us
    unnamed x2, local copies, waits for them, and re-layouts  3.2 us

profile of v2, /device:TPU:0, one launch (start us, length us, event | category | flops | bytes accessed | tf_op | source)
XLA Modules:
  0.0 126.0 jit_solution(4963119689031861543)
XLA Ops:
  0.6 122.1 %layer.1 = (bf16[64,2048]{1,0:T(8,128)(2,1)}, bf16[64,576]{1,0:T(8,128)(2,1)}) custom-call(s32[64]{0:T(128)} %refs_0_.1, s32[1,64]{1,0:T(1,128)} %bitcast.9, f32[1,128]{1,0:T(1,128)} %constant.2.clone.refs_2_, bf16[64,2048]{1,0:T(8,128)(2,1)} %refs_3_.1, s32[6,64]{1,0:T(8,128)} %bitcast.7, f32[6,64]{1,0:T(8,128)} %bitcast.8, bf16[64,576,256]{2,1,0:T(8,128)(2,1)} %bitcast.5, ...), custom_call_target="tpu_custom_call" | custom-call | tf_op jit(solution)/shard_map/layer/pallas_call | solution.py:468
  122.8 1.7 %copy.21 = bf16[64,2048]{1,0:T(8,128)(2,1)} copy(bf16[64,2048]{1,0:T(8,128)(2,1)} %get-tuple-element.4) | data formatting | bytes 524288
  124.4 1.5 %copy.22 = bf16[64,576]{1,0:T(8,128)(2,1)} copy(bf16[64,576]{1,0:T(8,128)(2,1)} %get-tuple-element.5) | data formatting | bytes 147456

commit v3 on v2

--- a/solution.py
+++ b/solution.py
@@ -13,10 +13,10 @@
 CAP_FACTOR = 2
 F32 = jnp.float32
 BF16 = jnp.bfloat16
-NSLOT = 5
-NCACHE = 6
+NSLOT = 6
+NCACHE = 5
 GROUP = 8
-NCHUNK = 4
+CHUNKS = (640, 640, 512, 256)
 MESH = pl.DeviceIdType.MESH
 
 
@@ -44,10 +44,10 @@
     return lax.broadcasted_iota(jnp.int32, shape, dim)
 
 
-def layer_kernel(cape, lens_s, lens_v, inv, x, ids, rw, cache, w_q, w_dkv, w_uk, w_uv, w_o, s_gate, s_up, s_down, e_gate, e_up, e_down,
+def layer_kernel(cape, lens, lens_row, inv_h, x_h, ids_h, rw_h, cache, w_q, w_dkv, w_uk, w_uv, w_o, s_gate, s_up, s_down, e_gate, e_up, e_down,
                  y, kvn,
-                 ring, cbuf, dkv_b, uk_b, uv_b, q_s, qf, kv_s, o_s, h1_s, u_all, gw_all, d_s, w_s, xr, acts, acts_sh, outs, rp, xs, rc, sh,
-                 ring_sem, c_sem, w_sem, gw_send, gw_recv, u_send, u_recv, p_send, p_recv, x_send, x_recv):
+                 lens_s, lens_v, inv, x, ids, rw, ring, cbuf, uk_b, uv_b, q_s, qf, kv_s, o_s, h1_s, u_all, gw_all, d_s, w_s, xr, acts, acts_sh, outs, rp, xs, rc, sh,
+                 in_sem, q_sem, ring_sem, c_sem, w_sem, gw_send, gw_recv, u_send, u_recv, p_send, p_recv, x_send, x_recv):
     bsz, hid = x.shape
     heads, nope, kvl = w_uk.shape
     kvd, lmax = cache.shape[1:]
@@ -57,10 +57,10 @@
     inter = e_gate.shape[2]
     n_dev = gw_all.shape[0] // bsz
     rows_e = n_dev * cape
-    cw = hid // NCHUNK
     grows = GROUP * heads
     nlat = kvl // 128
-    cb = cw // 128
+    nch = len(CHUNKS)
+    starts = [sum(CHUNKS[:j]) for j in range(nch)]
     me = lax.axis_index("ep")
 
     def peer(k):
@@ -76,10 +76,14 @@
             dst = ring.at[slot, pl.ds(0, rows), pl.ds(0, cols)]
         return pltpu.make_async_copy(src, dst, ring_sem.at[slot])
 
-    def wq_job(i):
-        a = i * inter
-        w = min(inter, w_q.shape[1] - a)
-        return to_slot(w_q.at[:, pl.ds(a, w)], i, hid, w)
+    wq_cols = []
+    for i in range(3):
+        for b, w in tiles(min(inter, w_q.shape[1] - i * inter), 768):
+            wq_cols.append((i, b, w))
+
+    def wq_job(p):
+        i, b, w = wq_cols[p]
+        return pltpu.make_async_copy(w_q.at[:, pl.ds(i * inter + b, w)], ring.at[i, :, pl.ds(b, w)], q_sem.at[p])
 
     def wo_job(i):
         a = i * inter
@@ -96,10 +100,9 @@
     def up_job(e):
         return to_slot(e_up.at[e], lax.rem(10 + 2 * e, NSLOT))
 
-    def down_job(i):
-        e = lax.rem(i, n_loc)
-        c = pl.multiple_of((i // n_loc) * cw, cw)
-        return to_slot(e_down.at[e, :, pl.ds(c, cw)], lax.rem(41 + i, NSLOT), inter, cw)
+    def down_job(j, e):
+        slot = lax.rem(41 + j * n_loc + e, NSLOT)
+        return to_slot(e_down.at[e, :, pl.ds(starts[j], CHUNKS[j])], slot, inter, CHUNKS[j])
 
     def sd_job(i):
         r = i % 2
@@ -111,18 +114,19 @@
         s = lax.rem(g, NCACHE)
         return pltpu.make_async_copy(cache.at[pl.ds(g * GROUP, GROUP)], cbuf.at[s], c_sem.at[s])
 
-    dkv_copy = pltpu.make_async_copy(w_dkv, dkv_b, w_sem.at[0])
+    dkv_a = inter - 256
+    dkv_copies = [pltpu.make_async_copy(w_dkv.at[:, pl.ds(0, dkv_a)], ring.at[2, pl.ds(0, kvd), pl.ds(256, dkv_a)], w_sem.at[0]),
+                  pltpu.make_async_copy(w_dkv.at[:, pl.ds(dkv_a, hid - dkv_a)], ring.at[2, pl.ds(kvd, kvd), pl.ds(256, hid - dkv_a)], w_sem.at[3])]
     uk_copy = pltpu.make_async_copy(w_uk, uk_b, w_sem.at[1])
     uv_copy = pltpu.make_async_copy(w_uv, uv_b, w_sem.at[2])
-    for i in range(3):
-        wq_job(i).start()
-    dkv_copy.start()
-    uk_copy.start()
-    for g in range(NCACHE):
-        cache_job(g).start()
-    uv_copy.start()
-    for i in range(2):
-        wo_job(i).start()
+    small = [pltpu.make_async_copy(a, b, in_sem.at[i]) for i, (a, b) in enumerate(
+        ((x_h, x), (lens, lens_s), (lens_row, lens_v), (inv_h, inv), (ids_h, ids), (rw_h, rw)))]
+    for c in small:
+        c.start()
+    for p in range(3):
+        wq_job(p).start()
+    for c in small:
+        c.wait()
 
     col = iota((bsz, 128), 1)
     expert = iota((128, bsz), 0)
@@ -155,19 +159,23 @@
     for k in range(1, n_dev):
         gw_copy(k).start()
 
-    for i in range(3):
-        wq_job(i).wait()
-        a = i * inter
-        for b, w in tiles(min(inter, w_q.shape[1] - a), 512):
-            q_s[:, a + b:a + b + w] = dot(xn, ring[i, :, b:b + w]).astype(BF16)
-    dkv_copy.wait()
-    kv = dot_nt(xn, dkv_b[...])
+    following = [[wq_job(3)], [wq_job(4)] + dkv_copies, [uk_copy, cache_job(0)], [cache_job(1)], [cache_job(2)]]
+    for p, (i, b, w) in enumerate(wq_cols):
+        wq_job(p).wait()
+        for c in following[p]:
+            c.start()
+        a = i * inter + b
+        q_s[:, a:a + w] = dot(xn, ring[i, :, b:b + w]).astype(BF16)
+    for c in dkv_copies:
+        c.wait()
+    kv = dot_nt(xn[:, :dkv_a], ring[2, :kvd, 256:]) + dot_nt(xn[:, dkv_a:], ring[2, kvd:2 * kvd, 256:256 + hid - dkv_a])
     kv_s[...] = jnp.zeros_like(kv_s)
     kv_s[:, :kvd] = kv
     kvn[:, :kvl] = rms(kv_s[:, :kvl]).astype(BF16)
     kvn[:, kvl:] = rope(kv_s[:, kvl:kvl + 128])[:, :kvd - kvl].astype(BF16)
 
     uk_copy.wait()
+    cache_job(3).start()
     left = col < 64
 
     def put_head(h, q_nope, q_rot):
@@ -187,6 +195,7 @@
         put_head(2 * hp + 1, jnp.where(left, r1, r2), r2)
 
     scale = qkd ** -0.5
+    n_groups = bsz // GROUP
     tpos = iota((heads, lmax), 1)
     seq_of_row = iota((grows, bsz), 0) // heads
     seq_col = iota((grows, bsz), 1)
@@ -194,6 +203,16 @@
     def attend(g, carry):
         s = lax.rem(g, NCACHE)
         cache_job(g).wait()
+
+        @pl.when(g + 4 < n_groups)
+        def _():
+            cache_job(g + 4).start()
+
+        for k, group in enumerate(([uv_copy, wo_job(0)], [wo_job(1)], [sgu_job(0)], [sgu_job(1)])):
+            @pl.when(g == n_groups - 4 + k)
+            def _():
+                for c in group:
+                    c.start()
         rows = pl.ds(pl.multiple_of(g * grows, grows), grows)
         qg = jnp.concatenate([qf[c, rows, :].astype(BF16) for c in range(nlat + 1)], axis=1)[:, :kvd]
         own = seq_col == seq_of_row + g * GROUP
@@ -215,20 +234,12 @@
         o_lat = jnp.concatenate(outs_i, axis=0) + o_new
         for c in range(nlat):
             qf[c, rows, :] = o_lat[:, 128 * c:128 * (c + 1)]
-
-        @pl.when(g + NCACHE < bsz // GROUP)
-        def _():
-            cache_job(g + NCACHE).start()
-
-        @pl.when(g == bsz // GROUP - NCACHE - 1)
-        def _():
-            for i in range(3):
-                sgu_job(i).start()
         return carry
 
-    lax.fori_loop(0, bsz // GROUP, attend, 0)
-
+    lax.fori_loop(0, n_groups, attend, 0)
+    sgu_job(2).start()
     uv_copy.wait()
+    sgu_job(3).start()
     for h in range(heads):
         oh = jnp.concatenate([qf[c, pl.ds(h, bsz, stride=heads), :].astype(BF16) for c in range(nlat)], axis=1)
         o_s[:, h * vh:(h + 1) * vh] = dot(oh, uv_b[h]).astype(BF16)
@@ -237,8 +248,8 @@
         a = i * inter
         for b, w in tiles(min(inter, hid - a), 512):
             h1_s[:, a + b:a + b + w] = (x[:, a + b:a + b + w].astype(F32) + dot(o_s[...], ring[3 + i, :, b:b + w])).astype(BF16)
-    sgu_job(3).start()
     gate_job(0).start()
+    up_job(0).start()
 
     u = rms(h1_s[...].astype(F32)).astype(BF16)
     mine = pl.ds(pl.multiple_of(me * bsz, bsz), bsz)
@@ -262,11 +273,11 @@
             acts_sh[:, i * inter + b:i * inter + b + w] = (silu(gg) * vv).astype(BF16)
 
     shared_gu(0)
-    up_job(0).start()
     gate_job(1).start()
+    up_job(1).start()
     shared_gu(1)
-    up_job(1).start()
     gate_job(2).start()
+    up_job(2).start()
 
     for k in range(1, n_dev):
         gw_copy(k).wait()
@@ -313,21 +324,15 @@
             vv = dot(xr[...], ring[su, :, b:b + w])
             acts[erows, b:b + w] = (silu(gg) * vv).astype(BF16)
 
-        @pl.when(e + 2 < n_loc)
-        def _():
-            up_job(e + 2).start()
-
-        @pl.when(e + 2 >= n_loc)
-        def _():
-            down_job(14 + 2 * e - 41).start()
-
         @pl.when(e + 3 < n_loc)
         def _():
             gate_job(e + 3).start()
+            up_job(e + 3).start()
 
         @pl.when(e + 3 >= n_loc)
         def _():
-            down_job(15 + 2 * e - 41).start()
+            down_job(0, 2 * (e + 3 - n_loc)).start()
+            down_job(0, 2 * (e + 3 - n_loc) + 1).start()
         return carry
 
     lax.fori_loop(0, n_loc, gate_up, 0)
@@ -335,12 +340,15 @@
     def part(j, d):
         return pl.ds(pl.multiple_of(j * nt + d * bsz, bsz), bsz)
 
+    def blocks(j):
+        return range(starts[j] // 128, (starts[j] + CHUNKS[j]) // 128)
+
     def pair_copy(j, i, d):
-        return pltpu.make_async_remote_copy(qf.at[pl.ds(0, cb), part(j, d)], rp.at[i, pl.ds(j * cb, cb)],
+        return pltpu.make_async_remote_copy(qf.at[pl.ds(0, len(blocks(j))), part(j, d)], rp.at[i, pl.ds(blocks(j)[0], len(blocks(j)))],
                                             p_send.at[j, i], p_recv.at[j, i], device_id={"ep": peer(1)}, device_id_type=MESH)
 
     def cross_copy(j):
-        blk = pl.ds(j * cb, cb)
+        blk = pl.ds(blocks(j)[0], len(blocks(j)))
         return pltpu.make_async_remote_copy(xs.at[blk], rc.at[blk], x_send.at[j], x_recv.at[j],
                                             device_id={"ep": peer(2)}, device_id_type=MESH)
 
@@ -350,22 +358,28 @@
 
     def forward(j):
         pair_copy(j, 1, peer(3)).wait_recv()
-        for c in range(cb):
-            xs[j * cb + c] = qf[c, part(j, peer(2)), :] + rp[1, j * cb + c]
+        for c, b in enumerate(blocks(j)):
+            xs[b] = qf[c, part(j, peer(2)), :] + rp[1, b]
         cross_copy(j).start()
 
-    for j in range(NCHUNK):
+    for j in range(nch):
+        cw = CHUNKS[j]
+
         def down(e, carry):
-            i = j * n_loc + e
-            down_job(i).wait()
+            down_job(j, e).wait()
             erows = pl.ds(pl.multiple_of(e * rows_e, rows_e), rows_e)
-            outs[erows, :] = dot(acts[erows, :], ring[lax.rem(41 + i, NSLOT), :inter, :cw]).astype(BF16)
-            if j < NCHUNK - 1:
-                down_job(i + NSLOT).start()
+            slot = lax.rem(41 + j * n_loc + e, NSLOT)
+            outs[erows, :cw] = dot(acts[erows, :], ring[slot, :inter, :cw]).astype(BF16)
+
+            @pl.when(e + NSLOT < n_loc)
+            def _():
+                down_job(j, e + NSLOT).start()
+
+            if j < nch - 1:
+                @pl.when(e + NSLOT >= n_loc)
+                def _():
+                    down_job(j + 1, e + NSLOT - n_loc).start()
             else:
-                @pl.when(e + NSLOT < n_loc)
-                def _():
-                    down_job(i + NSLOT).start()
                 for k in range(4):
                     @pl.when(e == n_loc - NSLOT + k)
                     def _():
@@ -375,11 +389,12 @@
         lax.fori_loop(0, n_loc, down, 0)
         if j >= 1:
             forward(j - 1)
-        ov = outs[...]
+        ov = outs[:, :cw]
         total = dot(w_s[0], ov) + dot(w_s[1], ov) + dot(w_s[2], ov)
-        for c in range(cb):
+        for c in range(cw // 128):
             qf[c, pl.ds(j * nt, nt), :] = total[:, 128 * c:128 * (c + 1)]
         start_pair(j)
+    forward(nch - 1)
 
     hw = hid // 2
     for c in range(2):
@@ -389,18 +404,15 @@
             acc = dot(acts_sh[:, :inter], ring[(105 + 2 * c) % NSLOT, :inter, b:b + w])
             acc += dot(acts_sh[:, inter:], ring[(106 + 2 * c) % NSLOT, :inter, b:b + w])
             sh[:, c * hw + b:c * hw + b + w] = acc
-        if c == 0:
-            forward(NCHUNK - 1)
-
-    for j in range(NCHUNK):
+
+    for j in range(nch):
         pair_copy(j, 0, peer(1)).wait_recv()
         cross_copy(j).wait_recv()
-        for c in range(cb):
-            b = j * cb + c
+        for c, b in enumerate(blocks(j)):
             cols = slice(b * 128, (b + 1) * 128)
             routed = qf[c, part(j, me), :] + rp[0, b] + rc[b]
             y[:, cols] = (h1_s[:, cols].astype(F32) + sh[:, cols] + routed).astype(BF16)
-    for j in range(NCHUNK):
+    for j in range(nch):
         pair_copy(j, 1, peer(3)).wait_send()
         pair_copy(j, 0, peer(1)).wait_send()
         cross_copy(j).wait_send()
@@ -423,7 +435,6 @@
         cape = (CAP_FACTOR * bsz * top + n_exp - 1) // n_exp
         rows_e = n * cape
         nt = n * bsz
-        cw = hid // NCHUNK
         half = (kvd - kvl) // 2
         inv = np.float64(ROPE_BASE) ** (-2.0 * (np.arange(128) % half) / (kvd - kvl))
         inv = jnp.asarray(inv.astype(np.float32)[None, :])
@@ -433,13 +444,18 @@
         call = pl.pallas_call(
             lambda *refs: layer_kernel(cape, *refs),
             name="layer",
-            out_shape=(jax.ShapeDtypeStruct((bsz, hid), BF16), jax.ShapeDtypeStruct((bsz, kvd), BF16)),
-            in_specs=[pl.BlockSpec(memory_space=pltpu.SMEM)] + [vm] * 5 + [hb] * 12,
+            out_shape=(pltpu.VMEM((bsz, hid), BF16), pltpu.VMEM((bsz, kvd), BF16)),
+            in_specs=[hb] * 18,
             out_specs=(vm, vm),
             scratch_shapes=[
+                pltpu.SMEM((bsz,), jnp.int32),
+                pltpu.VMEM((1, bsz), jnp.int32),
+                pltpu.VMEM((1, 128), F32),
+                pltpu.VMEM((bsz, hid), BF16),
+                pltpu.VMEM((top, bsz), jnp.int32),
+                pltpu.VMEM((top, bsz), F32),
                 pltpu.VMEM((NSLOT, hid, inter), BF16),
                 pltpu.VMEM((NCACHE, GROUP, kvd, lmax), BF16),
-                pltpu.VMEM(w_dkv.shape[::-1], BF16),
                 pltpu.VMEM(w_uk.shape, BF16),
                 pltpu.VMEM(w_uv.shape, BF16),
                 pltpu.VMEM((bsz, w_q.shape[1]), BF16),
@@ -454,16 +470,16 @@
                 pltpu.VMEM((rows_e, hid), BF16),
                 pltpu.VMEM((n_loc * rows_e, inter), BF16),
                 pltpu.VMEM((bsz, 2 * inter), BF16),
-                pltpu.VMEM((n_loc * rows_e, cw), BF16),
+                pltpu.VMEM((n_loc * rows_e, max(CHUNKS)), BF16),
                 pltpu.VMEM((2, hid // 128, bsz, 128), F32),
                 pltpu.VMEM((hid // 128, bsz, 128), F32),
                 pltpu.VMEM((hid // 128, bsz, 128), F32),
                 pltpu.VMEM((bsz, hid), F32),
-                dma((NSLOT,)), dma((NCACHE,)), dma((3,)),
+                dma((6,)), dma((5,)), dma((NSLOT,)), dma((NCACHE,)), dma((4,)),
                 dma((n - 1,)), dma((n - 1,)), dma((3,)), dma((3,)),
-                dma((NCHUNK, 2)), dma((NCHUNK, 2)), dma((NCHUNK,)), dma((NCHUNK,)),
+                dma((len(CHUNKS), 2)), dma((len(CHUNKS), 2)), dma((len(CHUNKS),)), dma((len(CHUNKS),)),
             ],
-            compiler_params=pltpu.CompilerParams(collective_id=0, has_side_effects=True, vmem_limit_bytes=67_043_328),
+            compiler_params=pltpu.CompilerParams(collective_id=0, has_side_effects=True, vmem_limit_bytes=66_600_000),
         )
         return call(lens, lens.reshape(1, bsz), inv, x, ids.T, rw.T, cache.transpose(0, 2, 1), w_q, w_dkv.T, w_uk, w_uv, w_o,
                     s_gate, s_up, s_down, e_gate, e_up, e_down)

time: 126 us -> 120 us (0.952)
  Pallas kernels: 122 us -> 118 us
  local copies, waits for them, and re-layouts: 3.2 us -> 1.34 us
    pallas_call x1, Pallas kernels: 122 us -> 118 us  [local(): call(lens, lens.reshape(1, bsz), inv, x, ids.T, rw.T, cache.transpose(0,...]
    unnamed x2, local copies, waits for them, and re-layouts: 3.2 us -> 1.34 us
where the time goes in v3:
time: 120 us
  Pallas kernels  118 us (98%)
  local copies, waits for them, and re-layouts  1.34 us (1%)
    pallas_call x1, Pallas kernels, local(): call(lens, lens.reshape(1, bsz), inv, x, ids.T, rw.T, cache.transpose(0,...  118 us

profile of v3, /device:TPU:0, one launch (start us, length us, event | category | flops | bytes accessed | tf_op | source)
XLA Modules:
  0.0 119.8 jit_solution(4367507980495832527)
XLA Ops:
  0.6 117.8 %layer.1 = (bf16[64,2048]{1,0:T(8,128)(2,1)S(1)}, bf16[64,576]{1,0:T(8,128)(2,1)S(1)}) custom-call(s32[64]{0:T(128)} %refs_0_.1, s32[1,64]{1,0:T(1,128)} %bitcast.9, f32[1,128]{1,0:T(1,128)} %constant.2.clone.refs_2_, bf16[64,2048]{1,0:T(8,128)(2,1)} %refs_3_.1, s32[6,64]{1,0:T(8,128)} %bitcast.7, f32[6,64]{1,0:T(8,128)} %bitcast.8, ...), custom_call_target="tpu_custom_call" | custom-call | tf_op jit(solution)/shard_map/layer/pallas_call | solution.py:484
  118.4 0.7 copy.21
  119.1 0.6 copy.22

commit v4 on v3

--- a/solution.py
+++ b/solution.py
@@ -16,7 +16,9 @@
 NSLOT = 6
 NCACHE = 5
 GROUP = 8
-CHUNKS = (640, 640, 512, 256)
+CHUNKS = (640, 640, 384, 256, 128)
+PACK = (1, 1, 2, 2, 4)
+PLACE = ((0, 0), (1, 0), (2, 0), (3, 0), (3, 2))
 MESH = pl.DeviceIdType.MESH
 
 
@@ -47,7 +49,7 @@
 def layer_kernel(cape, lens, lens_row, inv_h, x_h, ids_h, rw_h, cache, w_q, w_dkv, w_uk, w_uv, w_o, s_gate, s_up, s_down, e_gate, e_up, e_down,
                  y, kvn,
                  lens_s, lens_v, inv, x, ids, rw, ring, cbuf, uk_b, uv_b, q_s, qf, kv_s, o_s, h1_s, u_all, gw_all, d_s, w_s, xr, acts, acts_sh, outs, rp, xs, rc, sh,
-                 in_sem, q_sem, ring_sem, c_sem, w_sem, gw_send, gw_recv, u_send, u_recv, p_send, p_recv, x_send, x_recv):
+                 in_sem, q_sem, ring_sem, d_sem, c_sem, w_sem, gw_send, gw_recv, u_send, u_recv, p_send, p_recv, x_send, x_recv):
     bsz, hid = x.shape
     heads, nope, kvl = w_uk.shape
     kvd, lmax = cache.shape[1:]
@@ -61,6 +63,9 @@
     nlat = kvl // 128
     nch = len(CHUNKS)
     starts = [sum(CHUNKS[:j]) for j in range(nch)]
+    n_jobs = [n_loc // p for p in PACK]
+    base = [sum(n_jobs[:j]) for j in range(nch + 1)]
+    sd_base = 41 + base[nch]
     me = lax.axis_index("ep")
 
     def peer(k):
@@ -100,15 +105,21 @@
     def up_job(e):
         return to_slot(e_up.at[e], lax.rem(10 + 2 * e, NSLOT))
 
-    def down_job(j, e):
-        slot = lax.rem(41 + j * n_loc + e, NSLOT)
-        return to_slot(e_down.at[e, :, pl.ds(starts[j], CHUNKS[j])], slot, inter, CHUNKS[j])
+    def down_job(j, t):
+        slot = lax.rem(41 + base[j] + t, NSLOT)
+        return [pltpu.make_async_copy(e_down.at[t * PACK[j] + q, :, pl.ds(starts[j], CHUNKS[j])],
+                                      ring.at[slot, pl.ds(0, inter), pl.ds(q * CHUNKS[j], CHUNKS[j])],
+                                      ring_sem.at[slot] if PACK[j] == 1 else d_sem.at[slot, q]) for q in range(PACK[j])]
+
+    def start_down(j, t):
+        for c in down_job(j, t):
+            c.start()
 
     def sd_job(i):
         r = i % 2
         c = i // 2
         half = hid // 2
-        return to_slot(s_down.at[pl.ds(r * inter, inter), pl.ds(c * half, half)], (105 + i) % NSLOT, inter, half)
+        return to_slot(s_down.at[pl.ds(r * inter, inter), pl.ds(c * half, half)], (sd_base + i) % NSLOT, inter, half)
 
     def cache_job(g):
         s = lax.rem(g, NCACHE)
@@ -208,8 +219,8 @@
         def _():
             cache_job(g + 4).start()
 
-        for k, group in enumerate(([uv_copy, wo_job(0)], [wo_job(1)], [sgu_job(0)], [sgu_job(1)])):
-            @pl.when(g == n_groups - 4 + k)
+        for k, group in enumerate(([uv_copy], [wo_job(1)], [wo_job(0)], [sgu_job(0)], [sgu_job(1)], [sgu_job(2)], [sgu_job(3)])):
+            @pl.when(g == k)
             def _():
                 for c in group:
                     c.start()
@@ -237,9 +248,7 @@
         return carry
 
     lax.fori_loop(0, n_groups, attend, 0)
-    sgu_job(2).start()
     uv_copy.wait()
-    sgu_job(3).start()
     for h in range(heads):
         oh = jnp.concatenate([qf[c, pl.ds(h, bsz, stride=heads), :].astype(BF16) for c in range(nlat)], axis=1)
         o_s[:, h * vh:(h + 1) * vh] = dot(oh, uv_b[h]).astype(BF16)
@@ -331,20 +340,20 @@
 
         @pl.when(e + 3 >= n_loc)
         def _():
-            down_job(0, 2 * (e + 3 - n_loc)).start()
-            down_job(0, 2 * (e + 3 - n_loc) + 1).start()
+            start_down(0, 2 * (e + 3 - n_loc))
+            start_down(0, 2 * (e + 3 - n_loc) + 1)
         return carry
 
     lax.fori_loop(0, n_loc, gate_up, 0)
 
     def part(j, d):
-        return pl.ds(pl.multiple_of(j * nt + d * bsz, bsz), bsz)
+        return pl.ds(pl.multiple_of(PLACE[j][0] * nt + d * bsz, bsz), bsz)
 
     def blocks(j):
         return range(starts[j] // 128, (starts[j] + CHUNKS[j]) // 128)
 
     def pair_copy(j, i, d):
-        return pltpu.make_async_remote_copy(qf.at[pl.ds(0, len(blocks(j))), part(j, d)], rp.at[i, pl.ds(blocks(j)[0], len(blocks(j)))],
+        return pltpu.make_async_remote_copy(qf.at[pl.ds(PLACE[j][1], len(blocks(j))), part(j, d)], rp.at[i, pl.ds(blocks(j)[0], len(blocks(j)))],
                                             p_send.at[j, i], p_recv.at[j, i], device_id={"ep": peer(1)}, device_id_type=MESH)
 
     def cross_copy(j):
@@ -359,59 +368,65 @@
     def forward(j):
         pair_copy(j, 1, peer(3)).wait_recv()
         for c, b in enumerate(blocks(j)):
-            xs[b] = qf[c, part(j, peer(2)), :] + rp[1, b]
+            xs[b] = qf[PLACE[j][1] + c, part(j, peer(2)), :] + rp[1, b]
         cross_copy(j).start()
 
     for j in range(nch):
         cw = CHUNKS[j]
 
-        def down(e, carry):
-            down_job(j, e).wait()
-            erows = pl.ds(pl.multiple_of(e * rows_e, rows_e), rows_e)
-            slot = lax.rem(41 + j * n_loc + e, NSLOT)
-            outs[erows, :cw] = dot(acts[erows, :], ring[slot, :inter, :cw]).astype(BF16)
-
-            @pl.when(e + NSLOT < n_loc)
-            def _():
-                down_job(j, e + NSLOT).start()
-
-            if j < nch - 1:
-                @pl.when(e + NSLOT >= n_loc)
-                def _():
-                    down_job(j + 1, e + NSLOT - n_loc).start()
-            else:
-                for k in range(4):
-                    @pl.when(e == n_loc - NSLOT + k)
+        def down(t, carry):
+            for c in down_job(j, t):
+                c.wait()
+            slot = lax.rem(41 + base[j] + t, NSLOT)
+            for q in range(PACK[j]):
+                erows = pl.ds(pl.multiple_of((t * PACK[j] + q) * rows_e, rows_e), rows_e)
+                outs[erows, :cw] = dot(acts[erows, :], ring[slot, :inter, q * cw:(q + 1) * cw]).astype(BF16)
+            for j2 in range(j, nch):
+                first = base[j] + NSLOT - base[j2]
+                if first + n_jobs[j] > 0 and first < n_jobs[j2]:
+                    @pl.when((t + first >= 0) & (t + first < n_jobs[j2]))
+                    def _():
+                        start_down(j2, t + first)
+            for k in range(4):
+                if base[j] <= base[nch] + k - NSLOT < base[j + 1]:
+                    @pl.when(t == base[nch] + k - NSLOT - base[j])
                     def _():
                         sd_job(k).start()
+            if j >= 1:
+                @pl.when(t == n_jobs[j] // 2)
+                def _():
+                    forward(j - 1)
             return carry
 
-        lax.fori_loop(0, n_loc, down, 0)
-        if j >= 1:
-            forward(j - 1)
+        lax.fori_loop(0, n_jobs[j], down, 0)
         ov = outs[:, :cw]
         total = dot(w_s[0], ov) + dot(w_s[1], ov) + dot(w_s[2], ov)
         for c in range(cw // 128):
-            qf[c, pl.ds(j * nt, nt), :] = total[:, 128 * c:128 * (c + 1)]
+            qf[PLACE[j][1] + c, pl.ds(PLACE[j][0] * nt, nt), :] = total[:, 128 * c:128 * (c + 1)]
         start_pair(j)
     forward(nch - 1)
 
     hw = hid // 2
-    for c in range(2):
-        for r in range(2):
-            sd_job(2 * c + r).wait()
-        for b, w in tiles(hw, 512):
-            acc = dot(acts_sh[:, :inter], ring[(105 + 2 * c) % NSLOT, :inter, b:b + w])
-            acc += dot(acts_sh[:, inter:], ring[(106 + 2 * c) % NSLOT, :inter, b:b + w])
-            sh[:, c * hw + b:c * hw + b + w] = acc
-
-    for j in range(nch):
+
+    def finish(j):
         pair_copy(j, 0, peer(1)).wait_recv()
         cross_copy(j).wait_recv()
         for c, b in enumerate(blocks(j)):
             cols = slice(b * 128, (b + 1) * 128)
-            routed = qf[c, part(j, me), :] + rp[0, b] + rc[b]
+            routed = qf[PLACE[j][1] + c, part(j, me), :] + rp[0, b] + rc[b]
             y[:, cols] = (h1_s[:, cols].astype(F32) + sh[:, cols] + routed).astype(BF16)
+
+    for k in range(4):
+        c, r = k // 2, k % 2
+        if k == 3:
+            finish(0)
+        sd_job(k).wait()
+        for b, w in tiles(hw, 512):
+            cols = slice(c * hw + b, c * hw + b + w)
+            acc = dot(acts_sh[:, r * inter:(r + 1) * inter], ring[(sd_base + k) % NSLOT, :inter, b:b + w])
+            sh[:, cols] = acc if r == 0 else sh[:, cols] + acc
+    for j in range(1, nch):
+        finish(j)
     for j in range(nch):
         pair_copy(j, 1, peer(3)).wait_send()
         pair_copy(j, 0, peer(1)).wait_send()
@@ -475,7 +490,7 @@
                 pltpu.VMEM((hid // 128, bsz, 128), F32),
                 pltpu.VMEM((hid // 128, bsz, 128), F32),
                 pltpu.VMEM((bsz, hid), F32),
-                dma((6,)), dma((5,)), dma((NSLOT,)), dma((NCACHE,)), dma((4,)),
+                dma((6,)), dma((5,)), dma((NSLOT,)), dma((NSLOT, max(PACK))), dma((NCACHE,)), dma((4,)),
                 dma((n - 1,)), dma((n - 1,)), dma((3,)), dma((3,)),
                 dma((len(CHUNKS), 2)), dma((len(CHUNKS), 2)), dma((len(CHUNKS),)), dma((len(CHUNKS),)),
             ],

time: 120 us -> 116 us (0.967)
  Pallas kernels: 118 us -> 114 us
    pallas_call x1, Pallas kernels: 118 us -> 114 us  [local(): call(lens, lens.reshape(1, bsz), inv, x, ids.T, rw.T, cache.transpose(0,...]
where the time goes in v4:
time: 116 us
  Pallas kernels  114 us (98%)
  local copies, waits for them, and re-layouts  1.34 us (1%)
    pallas_call x1, Pallas kernels, local(): call(lens, lens.reshape(1, bsz), inv, x, ids.T, rw.T, cache.transpose(0,...  114 us

profile of v4, /device:TPU:0, one launch (start us, length us, event | category | flops | bytes accessed | tf_op | source)
XLA Modules:
  0.0 115.5 jit_solution(416644526187959159)
XLA Ops:
  0.6 113.5 %layer.1 = (bf16[64,2048]{1,0:T(8,128)(2,1)S(1)}, bf16[64,576]{1,0:T(8,128)(2,1)S(1)}) custom-call(s32[64]{0:T(128)} %refs_0_.1, s32[1,64]{1,0:T(1,128)} %bitcast.9, f32[1,128]{1,0:T(1,128)} %constant.2.clone.refs_2_, bf16[64,2048]{1,0:T(8,128)(2,1)} %refs_3_.1, s32[6,64]{1,0:T(8,128)} %bitcast.7, f32[6,64]{1,0:T(8,128)} %bitcast.8, ...), custom_call_target="tpu_custom_call" | custom-call | tf_op jit(solution)/shard_map/layer/pallas_call | solution.py:499
  114.2 0.7 copy.21
  114.9 0.6 copy.22

commit v5 on v4

--- a/solution.py
+++ b/solution.py
@@ -16,9 +16,9 @@
 NSLOT = 6
 NCACHE = 5
 GROUP = 8
-CHUNKS = (640, 640, 384, 256, 128)
-PACK = (1, 1, 2, 2, 4)
-PLACE = ((0, 0), (1, 0), (2, 0), (3, 0), (3, 2))
+CHUNKS = (256, 640, 640, 384, 128)
+PACK = (1, 1, 1, 2, 4)
+PLACE = ((3, 0), (0, 0), (1, 0), (2, 0), (3, 2))
 MESH = pl.DeviceIdType.MESH
 
 
@@ -49,10 +49,11 @@
 def layer_kernel(cape, lens, lens_row, inv_h, x_h, ids_h, rw_h, cache, w_q, w_dkv, w_uk, w_uv, w_o, s_gate, s_up, s_down, e_gate, e_up, e_down,
                  y, kvn,
                  lens_s, lens_v, inv, x, ids, rw, ring, cbuf, uk_b, uv_b, q_s, qf, kv_s, o_s, h1_s, u_all, gw_all, d_s, w_s, xr, acts, acts_sh, outs, rp, xs, rc, sh,
-                 in_sem, q_sem, ring_sem, d_sem, c_sem, w_sem, gw_send, gw_recv, u_send, u_recv, p_send, p_recv, x_send, x_recv):
+                 in_sem, q_sem, e_sem, ring_sem, d_sem, c_sem, w_sem, gw_send, gw_recv, u_send, u_recv, p_send, p_recv, x_send, x_recv):
     bsz, hid = x.shape
     heads, nope, kvl = w_uk.shape
-    kvd, lmax = cache.shape[1:]
+    kvd = w_dkv.shape[0]
+    lmax = cache.shape[1]
     qkd = nope + kvd - kvl
     vh = w_uv.shape[2]
     n_loc = e_gate.shape[0]
@@ -63,7 +64,7 @@
     nlat = kvl // 128
     nch = len(CHUNKS)
     starts = [sum(CHUNKS[:j]) for j in range(nch)]
-    n_jobs = [n_loc // p for p in PACK]
+    n_jobs = [0] + [n_loc // p for p in PACK[1:]]
     base = [sum(n_jobs[:j]) for j in range(nch + 1)]
     sd_base = 41 + base[nch]
     me = lax.axis_index("ep")
@@ -123,7 +124,11 @@
 
     def cache_job(g):
         s = lax.rem(g, NCACHE)
-        return pltpu.make_async_copy(cache.at[pl.ds(g * GROUP, GROUP)], cbuf.at[s], c_sem.at[s])
+        n = GROUP * kvd
+        return pltpu.make_async_copy(cache.at[pl.ds(pl.multiple_of(g * n, n), n)], cbuf.at[pl.ds(pl.multiple_of(s * n, n), n)], c_sem.at[s])
+
+    def early_down(e):
+        return pltpu.make_async_copy(e_down.at[e, :, pl.ds(0, CHUNKS[0])], cbuf.at[pl.ds(pl.multiple_of(e * inter, inter), inter)], e_sem.at[e])
 
     dkv_a = inter - 256
     dkv_copies = [pltpu.make_async_copy(w_dkv.at[:, pl.ds(0, dkv_a)], ring.at[2, pl.ds(0, kvd), pl.ds(256, dkv_a)], w_sem.at[0]),
@@ -211,6 +216,9 @@
     seq_of_row = iota((grows, bsz), 0) // heads
     seq_col = iota((grows, bsz), 1)
 
+    def seq_rows(s, i, n):
+        return pl.ds(pl.multiple_of((s * GROUP + i) * kvd, 64), n)
+
     def attend(g, carry):
         s = lax.rem(g, NCACHE)
         cache_job(g).wait()
@@ -230,7 +238,7 @@
         s_new = jnp.sum(jnp.where(own, dot_nt(qg, kvn[...]), 0.0), axis=1, keepdims=True) * scale
         parts = []
         for i in range(GROUP):
-            si = dot(qg[i * heads:(i + 1) * heads], cbuf[s, i]) * scale
+            si = dot(qg[i * heads:(i + 1) * heads], cbuf[seq_rows(s, i, kvd), :]) * scale
             parts.append(jnp.where(tpos < lens_s[g * GROUP + i], si, -jnp.inf))
         sc = jnp.concatenate(parts, axis=0)
         mx = jnp.maximum(jnp.max(sc, axis=1, keepdims=True), s_new)
@@ -241,7 +249,7 @@
         p = (e * rden).astype(BF16)
         p_new = jnp.where(own, e_new * rden, 0.0).astype(BF16)
         o_new = dot(p_new, kvn[:, :kvl])
-        outs_i = [dot_nt(p[i * heads:(i + 1) * heads], cbuf[s, i, :kvl, :]) for i in range(GROUP)]
+        outs_i = [dot_nt(p[i * heads:(i + 1) * heads], cbuf[seq_rows(s, i, kvl), :]) for i in range(GROUP)]
         o_lat = jnp.concatenate(outs_i, axis=0) + o_new
         for c in range(nlat):
             qf[c, rows, :] = o_lat[:, 128 * c:128 * (c + 1)]
@@ -249,9 +257,13 @@
 
     lax.fori_loop(0, n_groups, attend, 0)
     uv_copy.wait()
-    for h in range(heads):
-        oh = jnp.concatenate([qf[c, pl.ds(h, bsz, stride=heads), :].astype(BF16) for c in range(nlat)], axis=1)
-        o_s[:, h * vh:(h + 1) * vh] = dot(oh, uv_b[h]).astype(BF16)
+    def o_lat_of(h):
+        return jnp.concatenate([qf[c, pl.ds(h, bsz, stride=heads), :].astype(BF16) for c in range(nlat)], axis=1)
+
+    for h in range(0, heads, 2):
+        both = dot(jnp.concatenate([o_lat_of(h), o_lat_of(h + 1)], axis=0), jnp.concatenate([uv_b[h], uv_b[h + 1]], axis=1))
+        o_s[:, h * vh:(h + 1) * vh] = both[:bsz, :vh].astype(BF16)
+        o_s[:, (h + 1) * vh:(h + 2) * vh] = both[bsz:, vh:].astype(BF16)
     for i in range(2):
         wo_job(i).wait()
         a = i * inter
@@ -259,6 +271,12 @@
             h1_s[:, a + b:a + b + w] = (x[:, a + b:a + b + w].astype(F32) + dot(o_s[...], ring[3 + i, :, b:b + w])).astype(BF16)
     gate_job(0).start()
     up_job(0).start()
+
+    def start_early(e, carry):
+        early_down(e).start()
+        return carry
+
+    lax.fori_loop(0, n_loc, start_early, 0)
 
     u = rms(h1_s[...].astype(F32)).astype(BF16)
     mine = pl.ds(pl.multiple_of(me * bsz, bsz), bsz)
@@ -340,8 +358,11 @@
 
         @pl.when(e + 3 >= n_loc)
         def _():
-            start_down(0, 2 * (e + 3 - n_loc))
-            start_down(0, 2 * (e + 3 - n_loc) + 1)
+            start_down(1, 2 * (e + 3 - n_loc))
+            start_down(1, 2 * (e + 3 - n_loc) + 1)
+
+        early_down(e).wait()
+        outs[erows, :CHUNKS[0]] = dot(acts[erows, :], cbuf[pl.ds(pl.multiple_of(e * inter, inter), inter), :]).astype(BF16)
         return carry
 
     lax.fori_loop(0, n_loc, gate_up, 0)
@@ -398,7 +419,8 @@
                     forward(j - 1)
             return carry
 
-        lax.fori_loop(0, n_jobs[j], down, 0)
+        if j > 0:
+            lax.fori_loop(0, n_jobs[j], down, 0)
         ov = outs[:, :cw]
         total = dot(w_s[0], ov) + dot(w_s[1], ov) + dot(w_s[2], ov)
         for c in range(cw // 128):
@@ -418,14 +440,15 @@
 
     for k in range(4):
         c, r = k // 2, k % 2
-        if k == 3:
+        if k == 2:
             finish(0)
+            finish(1)
         sd_job(k).wait()
         for b, w in tiles(hw, 512):
             cols = slice(c * hw + b, c * hw + b + w)
             acc = dot(acts_sh[:, r * inter:(r + 1) * inter], ring[(sd_base + k) % NSLOT, :inter, b:b + w])
             sh[:, cols] = acc if r == 0 else sh[:, cols] + acc
-    for j in range(1, nch):
+    for j in range(2, nch):
         finish(j)
     for j in range(nch):
         pair_copy(j, 1, peer(3)).wait_send()
@@ -470,7 +493,7 @@
                 pltpu.VMEM((top, bsz), jnp.int32),
                 pltpu.VMEM((top, bsz), F32),
                 pltpu.VMEM((NSLOT, hid, inter), BF16),
-                pltpu.VMEM((NCACHE, GROUP, kvd, lmax), BF16),
+                pltpu.VMEM((NCACHE * GROUP * kvd, lmax), BF16),
                 pltpu.VMEM(w_uk.shape, BF16),
                 pltpu.VMEM(w_uv.shape, BF16),
                 pltpu.VMEM((bsz, w_q.shape[1]), BF16),
@@ -490,13 +513,13 @@
                 pltpu.VMEM((hid // 128, bsz, 128), F32),
                 pltpu.VMEM((hid // 128, bsz, 128), F32),
                 pltpu.VMEM((bsz, hid), F32),
-                dma((6,)), dma((5,)), dma((NSLOT,)), dma((NSLOT, max(PACK))), dma((NCACHE,)), dma((4,)),
+                dma((6,)), dma((5,)), dma((n_loc,)), dma((NSLOT,)), dma((NSLOT, max(PACK))), dma((NCACHE,)), dma((4,)),
                 dma((n - 1,)), dma((n - 1,)), dma((3,)), dma((3,)),
                 dma((len(CHUNKS), 2)), dma((len(CHUNKS), 2)), dma((len(CHUNKS),)), dma((len(CHUNKS),)),
             ],
             compiler_params=pltpu.CompilerParams(collective_id=0, has_side_effects=True, vmem_limit_bytes=66_600_000),
         )
-        return call(lens, lens.reshape(1, bsz), inv, x, ids.T, rw.T, cache.transpose(0, 2, 1), w_q, w_dkv.T, w_uk, w_uv, w_o,
+        return call(lens, lens.reshape(1, bsz), inv, x, ids.T, rw.T, cache.transpose(0, 2, 1).reshape(bsz * kvd, lmax), w_q, w_dkv.T, w_uk, w_uv, w_o,
                     s_gate, s_up, s_down, e_gate, e_up, e_down)
 
     in_specs = (row_spec, cache_spec, tok_spec, row_spec, row_spec) + (P(),) * 8 + (exp_spec,) * 3

time: 116 us -> 115 us (level)
  Pallas kernels: 114 us -> 112 us
where the time goes in v5:
time: 115 us; the launch traced here: 114 us
  Pallas kernels  112 us (97%)
  local copies, waits for them, and re-layouts  1.34 us (1%)
    pallas_call x1, Pallas kernels, local(): call(lens, lens.reshape(1, bsz), inv, x, ids.T, rw.T, cache.transpose(0,...  112 us

profile of v5, /device:TPU:0, one launch (start us, length us, event | category | flops | bytes accessed | tf_op | source)
XLA Modules:
  0.0 114.4 jit_solution(9381229370476581265)
XLA Ops:
  0.6 112.4 %layer.1 = (bf16[64,2048]{1,0:T(8,128)(2,1)S(1)}, bf16[64,576]{1,0:T(8,128)(2,1)S(1)}) custom-call(s32[64]{0:T(128)} %refs_0_.1, s32[1,64]{1,0:T(1,128)} %bitcast.11, f32[1,128]{1,0:T(1,128)} %constant.2.clone.refs_2_, bf16[64,2048]{1,0:T(8,128)(2,1)} %refs_3_.1, s32[6,64]{1,0:T(8,128)} %bitcast.9, f32[6,64]{1,0:T(8,128)} %bitcast.10, ...), custom_call_target="tpu_custom_call" | custom-call | tf_op jit(solution)/shard_map/layer/pallas_call | solution.py:522
  113.1 0.7 copy.21
  113.8 0.6 copy.22
